TPU v7x, 8 devices: a whole 2x2x1 slice. The times are simulated.
8 devices in a mesh: pod: 1 (over z), dp: 2 (over y), sp: 4 (over x, core).
Axes of the slice: x: 2, y: 2, z: 1, core: 2. Of those that a mesh axis runs over, the one named last changes fastest.
Arguments:
- images: bfloat16 [32, 48, 168, 128], P(('pod', 'dp'), 'sp')
- w_a: bfloat16 [2, 3, 3, 128, 128], replicated
- norm_a: float32 [2, 2, 128], replicated
- w_down: bfloat16 [3, 3, 128, 256], replicated
- norm_down: float32 [2, 256], replicated
- w_b: bfloat16 [1, 3, 3, 256, 256], replicated
- norm_b: float32 [1, 2, 256], replicated
Outputs:
- output: bfloat16 [32, 24, 84, 256], P(('pod', 'dp'), 'sp')
All inputs are finite; a program needn't handle non-finite values.
Results may differ from a plain program's by a relative error of at most 0.00496.
Values are sent between devices in bfloat16 or wider.
A program may use at most 1 GiB of HBM per device.

v0:
```python
import jax
import jax.numpy as jnp
from jax import lax
from jax.sharding import PartitionSpec as P

EPS_VALUE = 1e-5
CONV_DIMS = ('NHWC', 'HWIO', 'NHWC')


def solution(mesh):
    group_size = mesh.shape['sp']
    data_size = mesh.shape['dp']
    to_lower = [(dev_idx, dev_idx + 1) for dev_idx in range(group_size - 1)]
    to_upper = [(dev_idx + 1, dev_idx) for dev_idx in range(group_size - 1)]

    def batch_norm(z_val, norm_pair):
        local_sums = jnp.stack([jnp.sum(z_val, axis=(0, 1, 2)), jnp.sum(z_val * z_val, axis=(0, 1, 2))])
        group_sums = lax.psum(local_sums, ('dp', 'sp'))
        elem_count = z_val.shape[0] * z_val.shape[1] * z_val.shape[2] * data_size * group_size
        mean_val = group_sums[0] / elem_count
        var_val = group_sums[1] / elem_count - mean_val * mean_val
        scaled = norm_pair[0] * (z_val - mean_val) * lax.rsqrt(var_val + EPS_VALUE) + norm_pair[1]
        return jnp.maximum(scaled, 0.0).astype(jnp.bfloat16)

    def same_layer(hidden, weight, norm_pair):
        top_rows = lax.ppermute(hidden[:, -1:], 'sp', to_lower)
        bottom_rows = lax.ppermute(hidden[:, :1], 'sp', to_upper)
        padded = jnp.concatenate([top_rows, hidden, bottom_rows], axis=1)
        z_val = lax.conv_general_dilated(padded, weight, (1, 1), ((0, 0), (1, 1)), dimension_numbers=CONV_DIMS, preferred_element_type=jnp.float32)
        return batch_norm(z_val, norm_pair)

    def down_layer(hidden, weight, norm_pair):
        bottom_rows = lax.ppermute(hidden[:, :1], 'sp', to_upper)
        padded = jnp.concatenate([hidden, bottom_rows], axis=1)
        z_val = lax.conv_general_dilated(padded, weight, (2, 2), ((0, 0), (0, 1)), dimension_numbers=CONV_DIMS, preferred_element_type=jnp.float32)
        return batch_norm(z_val, norm_pair)

    def local_stack(row_tile, w_a, norm_a, w_down, norm_down, w_b, norm_b):
        hidden = row_tile
        for layer_idx in range(w_a.shape[0]):
            hidden = same_layer(hidden, w_a[layer_idx], norm_a[layer_idx])
        hidden = down_layer(hidden, w_down, norm_down)
        for layer_idx in range(w_b.shape[0]):
            hidden = same_layer(hidden, w_b[layer_idx], norm_b[layer_idx])
        return hidden

    act_spec = P(('pod', 'dp'), 'sp', None, None)
    return jax.shard_map(local_stack, mesh=mesh, in_specs=(act_spec, P(), P(), P(), P(), P(), P()), out_specs=act_spec, check_vma=False)
```

profile of v0, /device:TPU:0, one launch (start us, length us, event | category | flops | bytes accessed | tf_op | source)
XLA Modules:
  0.0 254.8 jit_solution(15919325666652883825)
XLA Ops:
  0.0 9.8 %copy.8 = bf16[16,12,168,128]{3,0,2,1:T(8,128)(2,1)} copy(bf16[16,12,168,128]{3,2,1,0:T(8,128)(2,1)} %param.7) | data formatting | bytes 16515072 | tf_op args[0]
  9.8 1.5 fusion.40
  11.4 2.8 %collective-permute-start = (bf16[16,1,168,128]{3,0,2,1:T(8,128)(2,1)S(1)}, bf16[16,1,168,128]{3,0,2,1:T(8,128)(2,1)S(1)}, u32[]{:S(2)}, u32[]{:S(2)}) collective-permute-start(bf16[16,1,168,128]{3,0,2,1:T(8,128)(2,1)S(1)} %get-tuple-element.15), channel_id=1, source_target_pairs={{0,1},{1,2},{2,3},{4,5},{5,6},{6,7}} | collective-permute-start | bytes 2064392 | tf_op jit(solution)/shard_map/ppermute | solution.py:26
  14.2 1.3 collective-permute-start.1
  15.5 0.4 collective-permute-done
  15.9 4.4 %collective-permute-done.1 = bf16[16,1,168,128]{3,0,2,1:T(8,128)(2,1)S(1)} collective-permute-done((bf16[16,1,168,128]{3,0,2,1:T(8,128)(2,1)S(1)}, bf16[16,1,168,128]{3,0,2,1:T(8,128)(2,1)S(1)}, u32[]{:S(2)}, u32[]{:S(2)}) %collective-permute-start.1) | collective-permute-done | bytes 688160 | tf_op jit(solution)/shard_map/ppermute | solution.py:27
  20.3 23.7 %fusion.36 = (f32[128]{0:T(128)S(1)}, f32[128]{0:T(128)S(1)}, f32[16,12,168,128]{3,0,2,1:T(8,128)}) fusion(bf16[2,3,3,128,128]{4,3,2,1,0:T(8,128)(2,1)S(1)} %copy-done.4, bf16[16,1,168,128]{3,0,2,1:T(8,128)(2,1)S(1)} %collective-permute-done.1, bf16[16,12,168,128]{3,0,2,1:T(8,128)(2,1)} %copy.8, bf16[16,1,168,128]{3,0,2,1:T(8,128)(2,1)S(1)} %collective-permute-done), kind=kOutput, calls=%fused_computation.62 | convolution fusion | flops 9516220416 | bytes 26444800 | tf_op jit(solution)/shard_map/conv_general_dilated | solution.py:29
  44.0 30.5 %psum.28 = f32[2,128]{1,0:T(2,128)S(1)} all-reduce(f32[2,128]{1,0:T(2,128)S(1)} %pad_maximum_fusion.2), channel_id=1, replica_groups=mesh['pod'=1,'dp'=2,'sp'=4] {'dp','sp'}, use_global_device_ids=true, to_apply=%region_2.0 | all-reduce | flops 256 | bytes 2048 | tf_op jit(solution)/shard_map/psum | solution.py:18
  74.5 7.6 %maximum_convert_fusion.1 = bf16[16,12,168,128]{3,0,2,1:T(8,128)(2,1)S(1)} fusion(f32[16,12,168,128]{3,0,2,1:T(8,128)} %get-tuple-element.31, f32[128]{0:T(128)S(1)} %get-tuple-element.30, f32[128]{0:T(128)S(1)} %fusion.30, f32[128]{0:T(128)S(1)} %multiply_bitcast_fusion.1, f32[128]{0:T(128)S(1)} %get-tuple-element.28), kind=kLoop, calls=%fused_computation.2 | loop fusion | flops 24772608 | bytes 24774656 | tf_op jit(solution)/shard_map/convert_element_type | solution.py:23
  82.1 0.2 fusion.39
  82.3 1.3 collective-permute-start.2
  83.7 1.5 collective-permute-start.3
  85.1 0.2 collective-permute-done.2
  85.4 4.8 %collective-permute-done.3 = bf16[16,1,168,128]{3,0,2,1:T(8,128)(2,1)S(1)} collective-permute-done((bf16[16,1,168,128]{3,0,2,1:T(8,128)(2,1)S(1)}, bf16[16,1,168,128]{3,0,2,1:T(8,128)(2,1)S(1)}, u32[]{:S(2)}, u32[]{:S(2)}) %collective-permute-start.3) | collective-permute-done | bytes 688160 | tf_op jit(solution)/shard_map/ppermute | solution.py:27
  90.2 22.6 %fusion.35 = (f32[128]{0:T(128)S(1)}, f32[128]{0:T(128)S(1)}, f32[16,12,168,128]{3,0,2,1:T(8,128)}) fusion(bf16[2,3,3,128,128]{4,3,2,1,0:T(8,128)(2,1)S(1)} %copy-done.4, bf16[16,1,168,128]{3,0,2,1:T(8,128)(2,1)S(1)} %collective-permute-done.3, bf16[16,12,168,128]{3,0,2,1:T(8,128)(2,1)S(1)} %maximum_convert_fusion.1, ...), kind=kOutput, calls=%fused_computation.61 | convolution fusion | flops 9516220416 | bytes 26444800 | tf_op jit(solution)/shard_map/conv_general_dilated | solution.py:29
  112.8 29.5 %psum.29 = f32[2,128]{1,0:T(2,128)S(1)} all-reduce(f32[2,128]{1,0:T(2,128)S(1)} %pad_maximum_fusion.3), channel_id=1, replica_groups=mesh['pod'=1,'dp'=2,'sp'=4] {'dp','sp'}, use_global_device_ids=true, to_apply=%region_5.0 | all-reduce | flops 256 | bytes 2048 | tf_op jit(solution)/shard_map/psum | solution.py:18
  142.3 0.0 copy-start.2
  142.3 7.6 %maximum_convert_fusion = bf16[16,12,168,128]{3,0,2,1:T(8,128)(2,1)S(1)} fusion(f32[16,12,168,128]{3,0,2,1:T(8,128)} %get-tuple-element.32, f32[128]{0:T(128)S(1)} %get-tuple-element.29, f32[128]{0:T(128)S(1)} %fusion.28, f32[128]{0:T(128)S(1)} %multiply_bitcast_fusion, f32[128]{0:T(128)S(1)} %get-tuple-element.27), kind=kLoop, calls=%fused_computation | loop fusion | flops 24772608 | bytes 24774656 | tf_op jit(solution)/shard_map/convert_element_type | solution.py:23
  149.9 0.1 slice.116
  150.0 1.3 collective-permute-start.4
  151.3 2.7 %collective-permute-done.4 = bf16[16,1,168,128]{3,0,2,1:T(8,128)(2,1)S(1)} collective-permute-done((bf16[16,1,168,128]{3,0,2,1:T(8,128)(2,1)S(1)}, bf16[16,1,168,128]{3,0,2,1:T(8,128)(2,1)S(1)}, u32[]{:S(2)}, u32[]{:S(2)}) %collective-permute-start.4) | collective-permute-done | bytes 688160 | tf_op jit(solution)/shard_map/ppermute | solution.py:33
  154.1 7.8 %fusion.38 = (f32[256]{0:T(256)S(1)}, f32[256]{0:T(256)S(1)}, f32[16,6,84,256]{3,0,2,1:T(8,128)}) fusion(bf16[3,3,128,256]{3,2,1,0:T(8,128)(2,1)S(1)} %copy-done.5, bf16[16,1,168,128]{3,0,2,1:T(8,128)(2,1)S(1)} %collective-permute-done.4, bf16[16,12,168,128]{3,0,2,1:T(8,128)(2,1)S(1)} %maximum_convert_fusion), kind=kOutput, calls=%fused_computation.64 | convolution fusion | flops 4761550848 | bytes 17795072 | tf_op jit(solution)/shard_map/conv_general_dilated | solution.py:35
  161.8 30.8 %psum.30 = f32[2,256]{1,0:T(2,128)S(1)} all-reduce(f32[2,256]{1,0:T(2,128)S(1)} %pad_maximum_fusion), channel_id=1, replica_groups=mesh['pod'=1,'dp'=2,'sp'=4] {'dp','sp'}, use_global_device_ids=true, to_apply=%region_8.0 | all-reduce | flops 512 | bytes 4096 | tf_op jit(solution)/shard_map/psum | solution.py:18
  192.7 4.9 %maximum_convert_fusion.3 = bf16[16,6,84,256]{3,0,2,1:T(8,128)(2,1)S(1)} fusion(f32[16,6,84,256]{3,0,2,1:T(8,128)} %get-tuple-element.33, f32[256]{0:T(256)S(1)} %bitcast.67, f32[256]{0:T(256)S(1)} %add_rsqrt_fusion.1, f32[256]{0:T(256)S(1)} %bitcast.61, f32[256]{0:T(256)S(1)} %bitcast.66), kind=kLoop, calls=%fused_computation.22 | loop fusion | flops 12386304 | bytes 12390400 | tf_op jit(solution)/shard_map/convert_element_type | solution.py:23
  197.6 0.1 fusion.41
  197.7 1.3 collective-permute-start.5
  199.0 1.3 collective-permute-start.6
  200.3 0.4 collective-permute-done.5
  200.7 4.8 %collective-permute-done.6 = bf16[16,1,84,256]{3,0,2,1:T(8,128)(2,1)S(1)} collective-permute-done((bf16[16,1,84,256]{3,0,2,1:T(8,128)(2,1)S(1)}, bf16[16,1,84,256]{3,0,2,1:T(8,128)(2,1)S(1)}, u32[]{:S(2)}, u32[]{:S(2)}) %collective-permute-start.6) | collective-permute-done | bytes 688160 | tf_op jit(solution)/shard_map/ppermute | solution.py:27
  205.5 12.9 %fusion.37 = (f32[256]{0:T(256)S(1)}, f32[256]{0:T(256)S(1)}, f32[16,6,84,256]{3,0,2,1:T(8,128)}) fusion(bf16[1,3,3,256,256]{4,3,2,1,0:T(8,128)(2,1)S(1)} %copy-done, bf16[16,1,84,256]{3,0,2,1:T(8,128)(2,1)S(1)} %collective-permute-done.6, bf16[16,6,84,256]{3,0,2,1:T(8,128)(2,1)S(1)} %maximum_convert_fusion.3, ...), kind=kOutput, calls=%fused_computation.63 | convolution fusion | flops 9459892224 | bytes 14944256 | tf_op jit(solution)/shard_map/conv_general_dilated | solution.py:29
  218.4 29.5 %psum.31 = f32[2,256]{1,0:T(2,128)S(1)} all-reduce(f32[2,256]{1,0:T(2,128)S(1)} %pad_maximum_fusion.1), channel_id=1, replica_groups=mesh['pod'=1,'dp'=2,'sp'=4] {'dp','sp'}, use_global_device_ids=true, to_apply=%region_11.0 | all-reduce | flops 512 | bytes 4096 | tf_op jit(solution)/shard_map/psum | solution.py:18
  247.9 6.9 %maximum_convert_fusion.2 = bf16[16,6,84,256]{3,0,2,1:T(8,128)(2,1)} fusion(f32[16,6,84,256]{3,0,2,1:T(8,128)} %get-tuple-element.34, f32[256]{0:T(256)S(1)} %bitcast.65, f32[256]{0:T(256)S(1)} %add_rsqrt_fusion, f32[256]{0:T(256)S(1)} %bitcast.63, f32[256]{0:T(256)S(1)} %bitcast.64), kind=kLoop, calls=%fused_computation.20 | loop fusion | flops 12386304 | bytes 12390400 | tf_op jit(solution)/shard_map/convert_element_type | solution.py:23
  (26 shorter events, 0.1 us)
Async XLA Ops:
  0.0 205.5 %copy-start = (bf16[1,3,3,256,256]{4,3,2,1,0:T(8,128)(2,1)S(1)}, bf16[1,3,3,256,256]{4,3,2,1,0:T(8,128)(2,1)}, u32[]{:S(2)}) copy-start(bf16[1,3,3,256,256]{4,3,2,1,0:T(8,128)(2,1)} %param.12) | copy-start | bytes 3538948
  0.0 15.5 %copy-start.1 = (f32[2,2,128]{2,1,0:T(2,128)S(1)}, f32[2,2,128]{2,1,0:T(2,128)}, u32[]{:S(2)}) copy-start(f32[2,2,128]{2,1,0:T(2,128)} %param.9) | copy-start | bytes 6148
  0.0 20.3 %copy-start.4 = (bf16[2,3,3,128,128]{4,3,2,1,0:T(8,128)(2,1)S(1)}, bf16[2,3,3,128,128]{4,3,2,1,0:T(8,128)(2,1)}, u32[]{:S(2)}) copy-start(bf16[2,3,3,128,128]{4,3,2,1,0:T(8,128)(2,1)} %param.8) | copy-start | bytes 1769476
  11.4 4.5 %collective-permute-start = (bf16[16,1,168,128]{3,0,2,1:T(8,128)(2,1)S(1)}, bf16[16,1,168,128]{3,0,2,1:T(8,128)(2,1)S(1)}, u32[]{:S(2)}, u32[]{:S(2)}) collective-permute-start(bf16[16,1,168,128]{3,0,2,1:T(8,128)(2,1)S(1)} %get-tuple-element.15), channel_id=1, source_target_pairs={{0,1},{1,2},{2,3},{4,5},{5,6},{6,7}} | collective-permute-start | bytes 2064392 | tf_op jit(solution)/shard_map/ppermute | solution.py:26
  14.2 6.1 %collective-permute-start.1 = (bf16[16,1,168,128]{3,0,2,1:T(8,128)(2,1)S(1)}, bf16[16,1,168,128]{3,0,2,1:T(8,128)(2,1)S(1)}, u32[]{:S(2)}, u32[]{:S(2)}) collective-permute-start(bf16[16,1,168,128]{3,0,2,1:T(8,128)(2,1)S(1)} %get-tuple-element.16), channel_id=1, source_target_pairs={{1,0},{2,1},{3,2},{5,4},{6,5},{7,6}} | collective-permute-start | bytes 2064392 | tf_op jit(solution)/shard_map/ppermute | solution.py:27
  82.3 3.1 %collective-permute-start.2 = (bf16[16,1,168,128]{3,0,2,1:T(8,128)(2,1)S(1)}, bf16[16,1,168,128]{3,0,2,1:T(8,128)(2,1)S(1)}, u32[]{:S(2)}, u32[]{:S(2)}) collective-permute-start(bf16[16,1,168,128]{3,0,2,1:T(8,128)(2,1)S(1)} %get-tuple-element.13), channel_id=1, source_target_pairs={{0,1},{1,2},{2,3},{4,5},{5,6},{6,7}} | collective-permute-start | bytes 2064392 | tf_op jit(solution)/shard_map/ppermute | solution.py:26
  83.7 6.5 %collective-permute-start.3 = (bf16[16,1,168,128]{3,0,2,1:T(8,128)(2,1)S(1)}, bf16[16,1,168,128]{3,0,2,1:T(8,128)(2,1)S(1)}, u32[]{:S(2)}, u32[]{:S(2)}) collective-permute-start(bf16[16,1,168,128]{3,0,2,1:T(8,128)(2,1)S(1)} %get-tuple-element.14), channel_id=1, source_target_pairs={{1,0},{2,1},{3,2},{5,4},{6,5},{7,6}} | collective-permute-start | bytes 2064392 | tf_op jit(solution)/shard_map/ppermute | solution.py:27
  142.3 9.1 %copy-start.2 = (f32[2,256]{1,0:T(2,128)S(1)}, f32[2,256]{1,0:T(2,128)}, u32[]{:S(2)}) copy-start(f32[2,256]{1,0:T(2,128)} %param.11) | copy-start | bytes 6148
  142.3 11.8 %copy-start.5 = (bf16[3,3,128,256]{3,2,1,0:T(8,128)(2,1)S(1)}, bf16[3,3,128,256]{3,2,1,0:T(8,128)(2,1)}, u32[]{:S(2)}) copy-start(bf16[3,3,128,256]{3,2,1,0:T(8,128)(2,1)} %param.10) | copy-start | bytes 1769476
  150.0 4.0 %collective-permute-start.4 = (bf16[16,1,168,128]{3,0,2,1:T(8,128)(2,1)S(1)}, bf16[16,1,168,128]{3,0,2,1:T(8,128)(2,1)S(1)}, u32[]{:S(2)}, u32[]{:S(2)}) collective-permute-start(bf16[16,1,168,128]{3,0,2,1:T(8,128)(2,1)S(1)} %slice.116), channel_id=1, source_target_pairs={{1,0},{2,1},{3,2},{5,4},{6,5},{7,6}} | collective-permute-start | bytes 2064392 | tf_op jit(solution)/shard_map/ppermute | solution.py:33
  161.8 38.5 %copy-start.3 = (f32[1,2,256]{2,1,0:T(2,128)S(1)}, f32[1,2,256]{2,1,0:T(2,128)}, u32[]{:S(2)}) copy-start(f32[1,2,256]{2,1,0:T(2,128)} %param.13) | copy-start | bytes 6148
  197.7 3.1 %collective-permute-start.5 = (bf16[16,1,84,256]{3,0,2,1:T(8,128)(2,1)S(1)}, bf16[16,1,84,256]{3,0,2,1:T(8,128)(2,1)S(1)}, u32[]{:S(2)}, u32[]{:S(2)}) collective-permute-start(bf16[16,1,84,256]{3,0,2,1:T(8,128)(2,1)S(1)} %get-tuple-element.17), channel_id=1, source_target_pairs={{0,1},{1,2},{2,3},{4,5},{5,6},{6,7}} | collective-permute-start | bytes 2064392 | tf_op jit(solution)/shard_map/ppermute | solution.py:26
  199.0 6.5 %collective-permute-start.6 = (bf16[16,1,84,256]{3,0,2,1:T(8,128)(2,1)S(1)}, bf16[16,1,84,256]{3,0,2,1:T(8,128)(2,1)S(1)}, u32[]{:S(2)}, u32[]{:S(2)}) collective-permute-start(bf16[16,1,84,256]{3,0,2,1:T(8,128)(2,1)S(1)} %get-tuple-element.18), channel_id=1, source_target_pairs={{1,0},{2,1},{3,2},{5,4},{6,5},{7,6}} | collective-permute-start | bytes 2064392 | tf_op jit(solution)/shard_map/ppermute | solution.py:27
where the time goes:
time: 256 us; the launch traced here: 255 us
  blocking collectives  120 us (47%)
  matrix products  66.9 us (26%)
  other arithmetic  27 us (11%)
  waiting for transfers between devices  17.7 us (7%)
  local copies, waits for them, and re-layouts  11.9 us (5%)
  starting transfers between devices  10.8 us (4%)
    psum x4, blocking collectives, batch_norm(): group_sums = lax.psum(local_sums, ('dp', 'sp'))  120 us
    conv_general_dilated x3, matrix products, same_layer(): lax.conv_general_dilated(padded, weight, (1, 1), ((0, 0), (1, 1)), dimens...  59.2 us
    convert_element_type x4, other arithmetic, batch_norm(): return jnp.maximum(scaled, 0.0).astype(jnp.bfloat16)  26.9 us
    ppermute x3, waiting for transfers between devices, same_layer(): bottom_rows = lax.ppermute(hidden[:, :1], 'sp', to_upper)  14 us
    unnamed x13, local copies, waits for them, and re-layouts  9.86 us
    conv_general_dilated x1, matrix products, down_layer(): lax.conv_general_dilated(padded, weight, (2, 2), ((0, 0), (0, 1)), dimens...  7.77 us
    ppermute x3, starting transfers between devices, same_layer(): top_rows = lax.ppermute(hidden[:, -1:], 'sp', to_lower)  5.48 us
  transfers between devices with their start and end apart: 7, of which 7 were waited for; matrix products, arithmetic and copies ran while one was open for 0% of the time, Pallas kernels for 0%

commit v1 on v0

v1 whole, which is shorter than its diff:
```python
import functools

import jax
import jax.numpy as jnp
from jax import lax
from jax.experimental import pallas as pl
from jax.experimental.pallas import tpu as pltpu
from jax.sharding import PartitionSpec as P

EPS_VALUE = 1e-5
F32 = jnp.float32
BF16 = jnp.bfloat16
MESH = pl.DeviceIdType.MESH

NIM = 16
ROWS = 12
COLS = 168
HALF = COLS // 2
MROW = HALF * NIM
YROW = (HALF + 1) * NIM
OROWS = 6
OCOLS = 84
OROW = OCOLS * NIM
O3ROW = (OCOLS + 2) * NIM
CHUNK = 336
GROUPS = 8


def kernel(x_ref, wa_ref, na_ref, wd_ref, nd_ref, wb_ref, nb_ref, out_ref,
           xs, tr, yy, zz, y3, z3, yo, wraw, wt, wdv, wbv, nav, ndv, nbv,
           st_out, st_in,
           x_sem, w_sem, xh_send, xh_recv, h2_send, h2_recv, h3_send, h3_recv, h4_send, h4_recv,
           st_send, st_recv, o_sem):
    dp = lax.axis_index("dp")
    sp = lax.axis_index("sp")
    me = dp * 4 + sp

    def x_copy(r):
        return pltpu.make_async_copy(x_ref.at[:, r], xs.at[r + 1], x_sem.at[r])
    w_copies = [
        pltpu.make_async_copy(wa_ref, wraw, w_sem.at[0]),
        pltpu.make_async_copy(wd_ref, wdv, w_sem.at[1]),
        pltpu.make_async_copy(wb_ref, wbv, w_sem.at[2]),
        pltpu.make_async_copy(na_ref, nav, w_sem.at[3]),
        pltpu.make_async_copy(nd_ref, ndv, w_sem.at[4]),
        pltpu.make_async_copy(nb_ref, nbv, w_sem.at[5]),
    ]
    w_copies[0].start()
    for r in (1, 2, 3, 4, 5, 6, 7, 8, 9, 10, 0, 11):
        x_copy(r).start()
    for c in w_copies[1:]:
        c.start()

    barrier = pltpu.get_barrier_semaphore()

    def peer(k):
        other = lax.rem(me + k, GROUPS)
        return (0, other // 4, lax.rem(other, 4))
    for k in range(1, GROUPS):
        pl.semaphore_signal(barrier, inc=1, device_id=peer(k), device_id_type=MESH)
    pl.semaphore_wait(barrier, GROUPS - 1)

    up = (0, dp, lax.rem(sp + 3, 4))
    down = (0, dp, lax.rem(sp + 1, 4))
    has_up = sp > 0
    has_down = sp < 3

    def halo(src_hi, dst_hi, src_lo, dst_lo, send, recv):
        hi = None if src_hi is None else pltpu.make_async_remote_copy(
            src_ref=src_hi, dst_ref=dst_hi, send_sem=send.at[0], recv_sem=recv.at[0],
            device_id=up, device_id_type=MESH)
        lo = None if src_lo is None else pltpu.make_async_remote_copy(
            src_ref=src_lo, dst_ref=dst_lo, send_sem=send.at[1], recv_sem=recv.at[1],
            device_id=down, device_id_type=MESH)

        def start():
            if hi is not None:
                @pl.when(has_up)
                def _():
                    hi.start()
            if lo is not None:
                @pl.when(has_down)
                def _():
                    lo.start()

        def wait_send():
            if hi is not None:
                @pl.when(has_up)
                def _():
                    hi.wait_send()
            if lo is not None:
                @pl.when(has_down)
                def _():
                    lo.wait_send()

        def wait_recv():
            if hi is not None:
                @pl.when(has_down)
                def _():
                    hi.wait_recv()
            if lo is not None:
                @pl.when(has_up)
                def _():
                    lo.wait_recv()
        return start, wait_send, wait_recv

    xh = halo(x_ref.at[:, 0], xs.at[ROWS + 1], x_ref.at[:, ROWS - 1], xs.at[0], xh_send, xh_recv)
    h2 = halo(yy.at[:, 1], yy.at[:, ROWS + 1], yy.at[:, ROWS], yy.at[:, 0], h2_send, h2_recv)
    h3 = halo(yy.at[:, 1], yy.at[:, ROWS + 1], None, None, h3_send, h3_recv)
    h4 = halo(y3.at[1], y3.at[OROWS + 1], y3.at[OROWS], y3.at[0], h4_send, h4_recv)

    xh[0]()

    zpad = jnp.zeros((NIM, 128), BF16)

    @pl.loop(0, ROWS + 2)
    def _(r):
        yy[0, r, pl.ds(0, NIM), :] = zpad
        yy[1, r, pl.ds(HALF * NIM, NIM), :] = zpad

    @pl.loop(0, OROWS + 2)
    def _(r):
        for c in (0, OCOLS + 1):
            y3[r, pl.ds(c * NIM, NIM), :] = jnp.zeros((NIM, 256), BF16)

    @pl.when(sp == 0)
    def _():
        for b in range(2):
            yy[b, 0] = jnp.zeros((YROW, 128), BF16)
        y3[0] = jnp.zeros((O3ROW, 256), BF16)

    @pl.when(sp == 3)
    def _():
        for b in range(2):
            yy[b, ROWS + 1] = jnp.zeros((YROW, 128), BF16)
        y3[OROWS + 1] = jnp.zeros((O3ROW, 256), BF16)

    w_copies[0].wait()
    zblk = jnp.zeros((128, 128), BF16)
    for layer in range(2):
        for q in range(3):
            k = 256 * q
            wt[layer, pl.ds(k, 128), pl.ds(0, 128)] = wraw[layer, 1, q]
            wt[layer, pl.ds(k, 128), pl.ds(128, 128)] = wraw[layer, 0, q]
            wt[layer, pl.ds(k + 128, 128), pl.ds(0, 128)] = wraw[layer, 2, q]
            wt[layer, pl.ds(k + 128, 128), pl.ds(128, 128)] = wraw[layer, 1, q]
            k = 768 + 256 * q
            wt[layer, pl.ds(k, 128), pl.ds(0, 128)] = wraw[layer, 0, q]
            wt[layer, pl.ds(k, 128), pl.ds(128, 128)] = zblk
            wt[layer, pl.ds(k + 128, 128), pl.ds(0, 128)] = zblk
            wt[layer, pl.ds(k + 128, 128), pl.ds(128, 128)] = wraw[layer, 2, q]
    for c in w_copies[1:]:
        c.wait()

    def transpose_row(r):
        for n in range(NIM):
            tr[pl.ds(n * COLS, COLS), :] = xs[r, n].astype(F32)
        for j in range(COLS):
            v = tr[pl.ds(j, NIM, stride=COLS), :].astype(BF16)
            b, a = (j + 1) % 2, (j + 1) // 2
            yy[b, r, pl.ds(a * NIM, NIM), :] = v

    def transpose_own(r):
        x_copy(r).wait()
        transpose_row(r + 1)

    @pl.loop(0, ROWS)
    def _(r):
        transpose_own(r)

    def exchange(layer, rows):
        buf = jnp.concatenate(rows + [jnp.zeros((8 - len(rows), 128), F32)], axis=0)
        st_out[layer] = buf
        st_in[layer, me] = buf
        copies = []
        for k in range(1, GROUPS):
            copies.append(pltpu.make_async_remote_copy(
                src_ref=st_out.at[layer], dst_ref=st_in.at[layer, me],
                send_sem=st_send.at[layer, k], recv_sem=st_recv.at[layer, k],
                device_id=peer(k), device_id_type=MESH))
        for c in copies:
            c.start()
        for c in copies:
            c.wait_recv()
        total = st_in[layer, 0]
        for s in range(1, GROUPS):
            total = total + st_in[layer, s]

        def finish():
            for c in copies:
                c.wait_send()
        return total, finish

    def moments(s1, s2, count):
        mean = s1 / count
        var = s2 / count - mean * mean
        return mean, lax.rsqrt(var + EPS_VALUE)

    def normalise(z, mean, inv, gamma, beta):
        return jnp.maximum(gamma * (z - mean) * inv + beta, 0.0).astype(BF16)

    TAPS = (((0, 0), (1, 0), (0, NIM)), ((1, 0), (0, NIM), (1, NIM)))

    def pair_layer(layer, before_border):
        def body(it, carry):
            s1, s2 = carry
            pair = jnp.where(it < 4, it + 1, (it - 4) * 5)
            i = pair * 2

            @pl.when(it == 4)
            def _():
                before_border()
            for b in range(2):
                for m in range(0, MROW, CHUNK):
                    parts = []
                    for rows in ((1, 2), (0, 3)):
                        for plane, off in TAPS[b]:
                            for rr in rows:
                                parts.append(yy[plane, i + rr, pl.ds(m + off, CHUNK), :])
                    lhs = jnp.concatenate(parts, axis=1)
                    res = jnp.dot(lhs, wt[layer], preferred_element_type=F32)
                    zz[b, i, pl.ds(m, CHUNK), :] = res[:, :128]
                    zz[b, i + 1, pl.ds(m, CHUNK), :] = res[:, 128:]
                    r3 = res.reshape(CHUNK // 8, 8, 256)
                    s1 = s1 + jnp.sum(r3, axis=0)
                    s2 = s2 + jnp.sum(r3 * r3, axis=0)
            return s1, s2
        zero = jnp.zeros((8, 256), F32)
        s1, s2 = lax.fori_loop(0, ROWS // 2, body, (zero, zero))
        s1 = jnp.sum(s1, axis=0, keepdims=True)
        s2 = jnp.sum(s2, axis=0, keepdims=True)
        total, finish = exchange(layer, [s1[:, :128] + s1[:, 128:], s2[:, :128] + s2[:, 128:]])
        mean, inv = moments(total[0:1], total[1:2], float(32 * 48 * 168))
        return mean, inv, finish

    def norm_row(r, mean, inv, gamma, beta):
        yy[1, r + 1, pl.ds(0, MROW), :] = normalise(zz[0, r], mean, inv, gamma, beta)
        yy[0, r + 1, pl.ds(NIM, MROW), :] = normalise(zz[1, r], mean, inv, gamma, beta)

    def first_border():
        xh[2]()

        @pl.when(has_up)
        def _():
            transpose_row(0)

        @pl.when(has_down)
        def _():
            transpose_row(ROWS + 1)

    mean, inv, fin1 = pair_layer(0, first_border)
    gamma, beta = nav[0, 0:1], nav[0, 1:2]

    @pl.loop(0, 2)
    def _(e):
        norm_row(e * (ROWS - 1), mean, inv, gamma, beta)
    h2[0]()

    @pl.loop(1, ROWS - 1)
    def _(r):
        norm_row(r, mean, inv, gamma, beta)

    mean2, inv2, fin2 = pair_layer(1, h2[2])
    gamma2, beta2 = nav[1, 0:1], nav[1, 1:2]
    h2[1]()
    norm_row(0, mean2, inv2, gamma2, beta2)
    h3[0]()

    @pl.loop(1, ROWS)
    def _(r):
        norm_row(r, mean2, inv2, gamma2, beta2)

    wd_taps = ((1, 0), (0, NIM), (1, NIM))

    def wide_layer(layer, n_it, row_of, lhs_of, w_val, before_last):
        def body(it, carry):
            s1, s2 = carry
            i = row_of(it)
            before_last(it)
            for m in range(0, OROW, CHUNK):
                lhs = jnp.concatenate(lhs_of(i, m), axis=1)
                res = jnp.dot(lhs, w_val, preferred_element_type=F32)
                z3[i, pl.ds(m, CHUNK), :] = res
                r3 = res.reshape(CHUNK // 8, 8, 256)
                s1 = s1 + jnp.sum(r3, axis=0)
                s2 = s2 + jnp.sum(r3 * r3, axis=0)
            return s1, s2
        zero = jnp.zeros((8, 256), F32)
        s1, s2 = lax.fori_loop(0, n_it, body, (zero, zero))
        s1 = jnp.sum(s1, axis=0, keepdims=True)
        s2 = jnp.sum(s2, axis=0, keepdims=True)
        total, finish = exchange(layer, [s1[:, :128], s1[:, 128:], s2[:, :128], s2[:, 128:]])
        s1 = jnp.concatenate([total[0:1], total[1:2]], axis=1)
        s2 = jnp.concatenate([total[2:3], total[3:4]], axis=1)
        mean, inv = moments(s1, s2, float(32 * 24 * 84))
        return mean, inv, finish

    def down_lhs(i, m):
        return [yy[plane, 2 * i + p + 1, pl.ds(m + off, CHUNK), :] for p in range(3) for plane, off in wd_taps]

    def down_border(it):
        @pl.when(it == OROWS - 1)
        def _():
            h3[2]()

    mean3, inv3, fin3 = wide_layer(2, OROWS, lambda it: it, down_lhs, wdv[...].reshape(9 * 128, 256), down_border)
    gamma3, beta3 = ndv[0:1], ndv[1:2]

    def norm3(r):
        y3[r + 1, pl.ds(NIM, OROW), :] = normalise(z3[r], mean3, inv3, gamma3, beta3)

    @pl.loop(0, 2)
    def _(e):
        norm3(e * (OROWS - 1))
    h4[0]()

    @pl.loop(1, OROWS - 1)
    def _(r):
        norm3(r)

    def last_lhs(i, m):
        return [y3[i + p, pl.ds(m + NIM * q, CHUNK), :] for p in range(3) for q in range(3)]

    def last_border(it):
        @pl.when(it == OROWS - 2)
        def _():
            h4[2]()

    mean4, inv4, fin4 = wide_layer(
        3, OROWS, lambda it: jnp.where(it < 4, it + 1, (it - 4) * 5), last_lhs,
        wbv[...].reshape(9 * 256, 256), last_border)
    gamma4, beta4 = nbv[0, 0:1], nbv[0, 1:2]

    def o_copy(r):
        return pltpu.make_async_copy(yo.at[r], out_ref.at[r], o_sem.at[r])

    @pl.loop(0, OROWS)
    def _(r):
        yo[r] = normalise(z3[r], mean4, inv4, gamma4, beta4)
        o_copy(r).start()

    xh[1]()
    h3[1]()
    h4[1]()
    for f in (fin1, fin2, fin3, fin4):
        f()

    @pl.loop(0, OROWS)
    def _(r):
        o_copy(r).wait()


def solution(mesh):
    any_spec = pl.BlockSpec(memory_space=pl.ANY)
    dma = pltpu.SemaphoreType.DMA

    def local_stack(images, w_a, norm_a, w_down, norm_down, w_b, norm_b):
        out = pl.pallas_call(
            kernel,
            out_shape=jax.ShapeDtypeStruct((OROWS, OROW, 256), BF16),
            in_specs=[any_spec] * 7,
            out_specs=any_spec,
            scratch_shapes=[
                pltpu.VMEM((ROWS + 2, NIM, COLS, 128), BF16),
                pltpu.VMEM((NIM * COLS, 128), F32),
                pltpu.VMEM((2, ROWS + 2, YROW, 128), BF16),
                pltpu.VMEM((2, ROWS, MROW, 128), F32),
                pltpu.VMEM((OROWS + 2, O3ROW, 256), BF16),
                pltpu.VMEM((OROWS, OROW, 256), F32),
                pltpu.VMEM((OROWS, OROW, 256), BF16),
                pltpu.VMEM((2, 3, 3, 128, 128), BF16),
                pltpu.VMEM((2, 1536, 256), BF16),
                pltpu.VMEM((3, 3, 128, 256), BF16),
                pltpu.VMEM((3, 3, 256, 256), BF16),
                pltpu.VMEM((2, 2, 128), F32),
                pltpu.VMEM((2, 256), F32),
                pltpu.VMEM((1, 2, 256), F32),
                pltpu.VMEM((4, 8, 128), F32),
                pltpu.VMEM((4, GROUPS, 8, 128), F32),
                dma((ROWS,)), dma((6,)),
                dma((2,)), dma((2,)), dma((2,)), dma((2,)), dma((2,)), dma((2,)), dma((2,)), dma((2,)),
                dma((4, GROUPS)), dma((4, GROUPS)), dma((OROWS,)),
            ],
            compiler_params=pltpu.CompilerParams(
                collective_id=0, has_side_effects=True, vmem_limit_bytes=67043328),
        )(images, w_a, norm_a, w_down, norm_down, w_b.reshape(3, 3, 256, 256), norm_b)
        return jnp.transpose(out.reshape(OROWS, OCOLS, NIM, 256), (2, 0, 1, 3))

    act_spec = P(('pod', 'dp'), 'sp', None, None)
    return jax.shard_map(local_stack, mesh=mesh, in_specs=(act_spec, P(), P(), P(), P(), P(), P()), out_specs=act_spec, check_vma=False)
```

time: 256 us -> 85.5 us (0.33)
  blocking collectives: 120 us -> 0 us
  Pallas kernels: 0 us -> 80.7 us
  matrix products: 66.9 us -> 0 us
  other arithmetic: 27 us -> 0 us
  waiting for transfers between devices: 17.7 us -> 0 us
  starting transfers between devices: 10.8 us -> 0 us
  local copies, waits for them, and re-layouts: 11.9 us -> 4.67 us
    psum x4 -> x0, blocking collectives: 120 us -> none  [batch_norm(): group_sums = lax.psum(local_sums, ('dp', 'sp'))]
    pallas_call x0 -> x1, Pallas kernels: none -> 80.7 us  [local_stack(): pl.pallas_call(kernel, out_shape=jax.ShapeDtypeStruct((OROWS, OROW, 256),...]
    conv_general_dilated x4 -> x0, matrix products: 66.9 us -> none  [the longest x3 59.2 us: same_layer(): lax.conv_general_dilated(padded, weight, (1, 1), ((0, 0), (1, 1)), dimens...]
    convert_element_type x4 -> x0, other arithmetic: 26.9 us -> none  [batch_norm(): return jnp.maximum(scaled, 0.0).astype(jnp.bfloat16)]
    ppermute x7 -> x0, waiting for transfers between devices: 17.7 us -> none  [the longest x3 14 us: same_layer(): bottom_rows = lax.ppermute(hidden[:, :1], 'sp', to_upper)]
    ppermute x7 -> x0, starting transfers between devices: 10.8 us -> none  [the longest x3 5.48 us: same_layer(): top_rows = lax.ppermute(hidden[:, -1:], 'sp', to_lower)]
    unnamed x13 -> x1, local copies, waits for them, and re-layouts: 9.86 us -> 4.67 us
  transfers between devices with their start and end apart: 7 -> 0, of which waited for: 7 -> 0; matrix products, arithmetic and copies ran while one was open for 0% -> 0% of each run, Pallas kernels for 0% -> 0%
where the time goes in v1:
time: 85.5 us; the launch traced here: 85.3 us
  Pallas kernels  80.7 us (94%)
  local copies, waits for them, and re-layouts  4.67 us (5%)
    pallas_call x1, Pallas kernels, local_stack(): pl.pallas_call(kernel, out_shape=jax.ShapeDtypeStruct((OROWS, OROW, 256),...  80.7 us
    unnamed x1, local copies, waits for them, and re-layouts  4.67 us

profile of v1, /device:TPU:0, one launch (start us, length us, event | category | flops | bytes accessed | tf_op | source)
XLA Modules:
  0.0 85.3 jit_solution(14063067307417105946)
XLA Ops:
  0.0 80.7 %shard_map.73 = bf16[6,1344,256]{2,1,0:T(8,128)(2,1)} custom-call(bf16[16,12,168,128]{3,2,1,0:T(8,128)(2,1)} %x_ref.1, bf16[2,3,3,128,128]{4,3,2,1,0:T(8,128)(2,1)} %wa_ref.1, f32[2,2,128]{2,1,0:T(2,128)} %na_ref.1, bf16[3,3,128,256]{3,2,1,0:T(8,128)(2,1)} %wd_ref.1, f32[2,256]{1,0:T(2,128)} %nd_ref.1, bf16[3,3,256,256]{3,2,1,0:T(8,128)(2,1)} %bitcast.5, ...), custom_call_target="tpu_custom_call" | custom-call | tf_op jit(solution)/shard_map/pallas_call | solution.py:358
  80.7 4.7 %copy.9 = bf16[16,6,84,256]{3,0,2,1:T(8,128)(2,1)} copy(bf16[16,6,84,256]{3,0,2,1:T(8,128)(2,1)} %bitcast.4) | data formatting | bytes 8257536

commit v2 on v0

v2 whole, which is shorter than its diff:
```python
import functools

import jax
import jax.numpy as jnp
from jax import lax
from jax.experimental import pallas as pl
from jax.experimental.pallas import tpu as pltpu
from jax.sharding import PartitionSpec as P

EPS_VALUE = 1e-5
F32 = jnp.float32
BF16 = jnp.bfloat16
MESH = pl.DeviceIdType.MESH

NIM = 16
ROWS = 12
COLS = 168
HALF = COLS // 2
MROW = HALF * NIM
YROW = (HALF + 1) * NIM
OROWS = 6
OCOLS = 84
OROW = OCOLS * NIM
O3ROW = (OCOLS + 2) * NIM
CHUNK = 336
VLIM = 59 * 1024 * 1024
GROUPS = 8


def kernel(x_ref, wa_ref, na_ref, wd_ref, nd_ref, wb_ref, nb_ref, out_ref,
           xs, tr, yy, zz, y3, z3, wraw, wt, wdv, wbv, nav, ndv, nbv,
           st_out, st_in,
           x_sem, w_sem, hx_send, hx_recv, h2_send, h2_recv, h3_send, h3_recv, h4_send, h4_recv,
           st_send, st_recv):
    dp = lax.axis_index("dp")
    sp = lax.axis_index("sp")
    me = dp * 4 + sp
    flip = 1 - lax.rem(sp, 2)
    near = (0, dp, sp + 2 * flip - 1)
    far = (0, dp, lax.rem(7 - sp, 4))
    has_far = jnp.logical_or(sp == 1, sp == 2)

    def x_row(r):
        return r + flip * (ROWS - 1 - 2 * r)

    def tap(p):
        return p + flip * (2 - 2 * p)

    def x_copy(r):
        return pltpu.make_async_copy(x_ref.at[:, x_row(r)], xs.at[r + 1], x_sem.at[r])
    wa_copies = [pltpu.make_async_copy(wa_ref.at[l, tap(p)], wraw.at[l, p], w_sem.at[3 * l + p])
                 for l in range(2) for p in range(3)]
    w_copies = [pltpu.make_async_copy(na_ref, nav, w_sem.at[6]),
                pltpu.make_async_copy(nd_ref, ndv, w_sem.at[7]),
                pltpu.make_async_copy(nb_ref, nbv, w_sem.at[8])]
    for p in range(3):
        w_copies.append(pltpu.make_async_copy(wd_ref.at[tap(p)], wdv.at[p], w_sem.at[9 + p]))
        w_copies.append(pltpu.make_async_copy(wb_ref.at[tap(p)], wbv.at[p], w_sem.at[12 + p]))

    barrier = pltpu.get_barrier_semaphore()

    def peer(k):
        other = lax.rem(me + k, GROUPS)
        return (0, other // 4, lax.rem(other, 4))
    for k in range(1, GROUPS):
        pl.semaphore_signal(barrier, inc=1, device_id=peer(k), device_id_type=MESH)

    for r in range(3):
        x_copy(r).start()
    for c in wa_copies:
        c.start()
    for r in range(3, ROWS):
        x_copy(r).start()
    for c in w_copies:
        c.start()

    def halo(src_near, dst_near, src_far, dst_far, send, recv):
        n_copy = pltpu.make_async_remote_copy(
            src_ref=src_near, dst_ref=dst_near, send_sem=send.at[0], recv_sem=recv.at[0],
            device_id=near, device_id_type=MESH)
        f_copy = pltpu.make_async_remote_copy(
            src_ref=src_far, dst_ref=dst_far, send_sem=send.at[1], recv_sem=recv.at[1],
            device_id=far, device_id_type=MESH)
        return n_copy, f_copy

    hx_near, hx_far = halo(x_ref.at[:, x_row(0)], xs.at[0], x_ref.at[:, x_row(ROWS - 1)], xs.at[ROWS + 1],
                           hx_send, hx_recv)
    h2_near, h2_far = halo(yy.at[:, 1], yy.at[:, 0], yy.at[:, ROWS], yy.at[:, ROWS + 1], h2_send, h2_recv)
    h3_near, h3_far = halo(yy.at[:, 1], yy.at[:, 0], yy.at[:, ROWS], yy.at[:, ROWS + 1], h3_send, h3_recv)
    h4_near, h4_far = halo(y3.at[1], y3.at[0], y3.at[OROWS], y3.at[OROWS + 1], h4_send, h4_recv)

    zpad = jnp.zeros((NIM, 128), BF16)

    @pl.loop(0, ROWS + 2)
    def _(r):
        yy[0, r, pl.ds(0, NIM), :] = zpad
        yy[1, r, pl.ds(HALF * NIM, NIM), :] = zpad

    @pl.loop(0, OROWS + 2)
    def _(r):
        for c in (0, OCOLS + 1):
            y3[r, pl.ds(c * NIM, NIM), :] = jnp.zeros((NIM, 256), BF16)

    @pl.when(jnp.logical_not(has_far))
    def _():
        for b in range(2):
            yy[b, ROWS + 1] = jnp.zeros((YROW, 128), BF16)
        y3[OROWS + 1] = jnp.zeros((O3ROW, 256), BF16)

    def transpose_row(r):
        for n in range(NIM):
            tr[pl.ds(n * COLS, COLS), :] = xs[r, n].astype(F32)
        for j in range(COLS):
            v = tr[pl.ds(j, NIM, stride=COLS), :].astype(BF16)
            b, a = (j + 1) % 2, (j + 1) // 2
            yy[b, r, pl.ds(a * NIM, NIM), :] = v

    with jax.named_scope('transpose'):
        @pl.loop(0, 3)
        def _(r):
            x_copy(r).wait()
            transpose_row(r + 1)

    with jax.named_scope('barrier'):
        pl.semaphore_wait(barrier, GROUPS - 1)
    hx_near.start()

    @pl.when(has_far)
    def _():
        hx_far.start()

    for c in wa_copies:
        c.wait()
    zblk = jnp.zeros((128, 128), BF16)
    for layer in range(2):
        def put(k, lo, hi):
            wt[layer, pl.ds(k, 128), pl.ds(0, 128)] = zblk if lo is None else wraw[layer, lo[0], lo[1]]
            wt[layer, pl.ds(k, 128), pl.ds(128, 128)] = zblk if hi is None else wraw[layer, hi[0], hi[1]]
        for q in range(3):
            put(256 * q, (1, q), (0, q))
            put(256 * q + 128, (2, q), (1, q))
        for e, p in enumerate((0, 2)):
            k = 768 + 512 * e
            put(k, (p, 0), None)
            put(k + 128, (p, 1), (p, 0))
            put(k + 256, (p, 2), (p, 1))
            put(k + 384, None, (p, 2))

    with jax.named_scope('transpose2'):
        @pl.loop(3, 6)
        def _(r):
            x_copy(r).wait()
            transpose_row(r + 1)
    for c in w_copies:
        c.wait()

    def exchange(layer, rows):
        buf = jnp.concatenate(rows + [jnp.zeros((8 - len(rows), 128), F32)], axis=0)
        st_out[layer] = buf
        st_in[layer, me] = buf
        copies = []
        for k in range(1, GROUPS):
            copies.append(pltpu.make_async_remote_copy(
                src_ref=st_out.at[layer], dst_ref=st_in.at[layer, me],
                send_sem=st_send.at[layer, k], recv_sem=st_recv.at[layer, k],
                device_id=peer(k), device_id_type=MESH))
        for c in copies:
            c.start()
        with jax.named_scope(f'stat{layer}'):
            for c in copies:
                c.wait_recv()
        total = st_in[layer, 0]
        for s in range(1, GROUPS):
            total = total + st_in[layer, s]

        def finish():
            for c in copies:
                c.wait_send()
        return total, finish

    def moments(s1, s2, count):
        mean = s1 / count
        var = s2 / count - mean * mean
        return mean, lax.rsqrt(var + EPS_VALUE)

    def normalise(z, mean, inv, gamma, beta):
        return jnp.maximum(gamma * (z - mean) * inv + beta, 0.0).astype(BF16)

    TAPS = (((0, 0), (1, 0), (0, NIM)), ((1, 0), (0, NIM), (1, NIM)))
    QUAD = ((0, 0), (1, 0), (0, NIM), (1, NIM))

    def pair_layer(layer, ahead, before):
        def conv(i, carry):
            s1, s2 = carry
            for m in range(0, MROW, CHUNK):
                def take(taps, rows):
                    return jnp.concatenate(
                        [yy[plane, i + rr, pl.ds(m + off, CHUNK), :] for plane, off in taps for rr in rows], axis=1)
                mid = [jnp.dot(take(TAPS[b], (1, 2)), wt[layer, pl.ds(0, 768), :], preferred_element_type=F32)
                       for b in range(2)]
                edge = [jnp.dot(take(QUAD, (3 * e,)), wt[layer, pl.ds(768 + 512 * e, 512), :],
                                preferred_element_type=F32) for e in range(2)]
                for b in range(2):
                    for e in range(2):
                        z = mid[b][:, 128 * e:128 * e + 128] + edge[e][:, 128 * b:128 * b + 128]
                        zz[b, i + e, pl.ds(m, CHUNK), :] = z
                        z8 = z.reshape(CHUNK // 8, 8, 128)
                        s1 = s1 + jnp.sum(z8, axis=0)
                        s2 = s2 + jnp.sum(z8 * z8, axis=0)
            return s1, s2

        def first(it, carry):
            i = 2 * it
            if before is not None:
                before(it)
            ahead(i)
            return conv(i, carry)

        def second(it, carry):
            pair = jnp.where(it == 0, 4, (it - 1) * 5)

            @pl.when(it == 1)
            def _():
                with jax.named_scope(f'near{layer}'):
                    border_near(layer)

            @pl.when(it == 2)
            def _():
                with jax.named_scope(f'far{layer}'):
                    border_far(layer)
            return conv(2 * pair, carry)

        zero = jnp.zeros((8, 128), F32)
        with jax.named_scope(f'pairA{layer}'):
            carry = lax.fori_loop(1, 4, first, (zero, zero))
        with jax.named_scope(f'pairB{layer}'):
            s1, s2 = lax.fori_loop(0, 3, second, carry)
        total, finish = exchange(layer, [jnp.sum(s1, axis=0, keepdims=True), jnp.sum(s2, axis=0, keepdims=True)])
        mean, inv = moments(total[0:1], total[1:2], float(32 * 48 * 168))
        return mean, inv, finish

    def border_near(layer):
        if layer == 0:
            hx_near.wait_recv()
            transpose_row(0)
        else:
            h2_near.wait_recv()

    def border_far(layer):
        @pl.when(has_far)
        def _():
            if layer == 0:
                hx_far.wait_recv()
                transpose_row(ROWS + 1)
            else:
                h2_far.wait_recv()

    def norm_row(r, mean, inv, gamma, beta):
        yy[1, r + 1, pl.ds(0, MROW), :] = normalise(zz[0, r], mean, inv, gamma, beta)
        yy[0, r + 1, pl.ds(NIM, MROW), :] = normalise(zz[1, r], mean, inv, gamma, beta)

    def first_before(it):
        for e in range(2):
            x_copy(2 * it + 4 + e).wait()

    def first_ahead(i):
        transpose_row(i + 5)
        transpose_row(i + 6)

    mean, inv, fin1 = pair_layer(0, first_ahead, first_before)
    gamma, beta = nav[0, 0:1], nav[0, 1:2]

    with jax.named_scope('norm1'):
        norm_row(ROWS - 1, mean, inv, gamma, beta)

        @pl.when(has_far)
        def _():
            h2_far.start()
        norm_row(0, mean, inv, gamma, beta)
        h2_near.start()

        @pl.loop(1, 5)
        def _(r):
            norm_row(r, mean, inv, gamma, beta)

    def second_ahead(i):
        norm_row(i + 3, mean, inv, gamma, beta)
        norm_row(i + 4, mean, inv, gamma, beta)

    mean2, inv2, fin2 = pair_layer(1, second_ahead, None)
    gamma2, beta2 = nav[1, 0:1], nav[1, 1:2]
    h2_near.wait_send()

    @pl.when(has_far)
    def _():
        h2_far.wait_send()

    sends_near = flip == 0
    sends_far = sp == 2
    with jax.named_scope('norm2'):
        norm_row((ROWS - 1) * flip, mean2, inv2, gamma2, beta2)

        @pl.when(sends_near)
        def _():
            h3_near.start()

        @pl.when(sends_far)
        def _():
            h3_far.start()

        @pl.loop(1, ROWS)
        def _(r):
            norm_row(r - flip, mean2, inv2, gamma2, beta2)

    wd_taps = ((1, 0), (0, NIM), (1, NIM))

    def wide_conv(i, lhs_of, w_val, carry):
        s1, s2 = carry
        for m in range(0, OROW, CHUNK):
            lhs = jnp.concatenate(lhs_of(i, m), axis=1)
            res = jnp.dot(lhs, w_val, preferred_element_type=F32)
            z3[i, pl.ds(m, CHUNK), :] = res
            r3 = res.reshape(CHUNK // 8, 8, 256)
            s1 = s1 + jnp.sum(r3, axis=0)
            s2 = s2 + jnp.sum(r3 * r3, axis=0)
        return s1, s2

    def wide_stats(layer, carry):
        s1, s2 = carry
        s1 = jnp.sum(s1, axis=0, keepdims=True)
        s2 = jnp.sum(s2, axis=0, keepdims=True)
        total, finish = exchange(layer, [s1[:, :128], s1[:, 128:], s2[:, :128], s2[:, 128:]])
        s1 = jnp.concatenate([total[0:1], total[1:2]], axis=1)
        s2 = jnp.concatenate([total[2:3], total[3:4]], axis=1)
        mean, inv = moments(s1, s2, float(32 * 24 * 84))
        return mean, inv, finish

    zero = jnp.zeros((8, 256), F32)

    def down_lhs(i, m):
        return [yy[plane, 2 * i - flip + p + 1, pl.ds(m + off, CHUNK), :] for p in range(3) for plane, off in wd_taps]

    def down_body(it, carry):
        @pl.when(it == OROWS - 1)
        def _():
            with jax.named_scope('halo2'):
                @pl.when(flip == 1)
                def _():
                    h3_near.wait_recv()

                @pl.when(sp == 1)
                def _():
                    h3_far.wait_recv()
        return wide_conv(lax.rem(it + flip, OROWS), down_lhs, wdv[...].reshape(9 * 128, 256), carry)

    with jax.named_scope('wide2'):
        carry = lax.fori_loop(0, OROWS, down_body, (zero, zero))
    mean3, inv3, fin3 = wide_stats(2, carry)
    gamma3, beta3 = ndv[0:1], ndv[1:2]

    def norm3(r):
        y3[r + 1, pl.ds(NIM, OROW), :] = normalise(z3[r], mean3, inv3, gamma3, beta3)

    with jax.named_scope('norm3'):
        norm3(OROWS - 1)

        @pl.when(has_far)
        def _():
            h4_far.start()
        norm3(0)
        h4_near.start()

        @pl.loop(1, 3)
        def _(r):
            norm3(r)

    def last_lhs(i, m):
        return [y3[i + p, pl.ds(m + NIM * q, CHUNK), :] for p in range(3) for q in range(3)]

    wb_val = wbv[...].reshape(9 * 256, 256)

    def last_first(it, carry):
        norm3(it + 2)
        return wide_conv(it, last_lhs, wb_val, carry)

    def last_second(it, carry):
        i = jnp.where(it < 2, it + 3, (it - 2) * 5)

        @pl.when(it == 2)
        def _():
            with jax.named_scope('near3'):
                h4_near.wait_recv()

        @pl.when(it == 3)
        def _():
            with jax.named_scope('far3'):
                @pl.when(has_far)
                def _():
                    h4_far.wait_recv()
        return wide_conv(i, last_lhs, wb_val, carry)

    with jax.named_scope('wide3A'):
        carry = lax.fori_loop(1, 3, last_first, (zero, zero))
    with jax.named_scope('wide3B'):
        carry = lax.fori_loop(0, 4, last_second, carry)
    mean4, inv4, fin4 = wide_stats(3, carry)
    gamma4, beta4 = nbv[0, 0:1], nbv[0, 1:2]

    with jax.named_scope('out'):
        @pl.loop(0, OROWS)
        def _(r):
            out_ref[r + flip * (OROWS - 1 - 2 * r)] = normalise(z3[r], mean4, inv4, gamma4, beta4)

    with jax.named_scope('drain'):
        hx_near.wait_send()
        h4_near.wait_send()

        @pl.when(has_far)
        def _():
            hx_far.wait_send()
            h4_far.wait_send()

        @pl.when(sends_near)
        def _():
            h3_near.wait_send()

        @pl.when(sends_far)
        def _():
            h3_far.wait_send()
        for f in (fin1, fin2, fin3, fin4):
            f()


def solution(mesh):
    any_spec = pl.BlockSpec(memory_space=pl.ANY)
    dma = pltpu.SemaphoreType.DMA

    def local_stack(images, w_a, norm_a, w_down, norm_down, w_b, norm_b):
        out = pl.pallas_call(
            kernel,
            out_shape=pltpu.VMEM((OROWS, OROW, 256), BF16),
            in_specs=[any_spec] * 7,
            out_specs=pl.BlockSpec(memory_space=pltpu.VMEM),
            scratch_shapes=[
                pltpu.VMEM((ROWS + 2, NIM, COLS, 128), BF16),
                pltpu.VMEM((NIM * COLS, 128), F32),
                pltpu.VMEM((2, ROWS + 2, YROW, 128), BF16),
                pltpu.VMEM((2, ROWS, MROW, 128), F32),
                pltpu.VMEM((OROWS + 2, O3ROW, 256), BF16),
                pltpu.VMEM((OROWS, OROW, 256), F32),
                pltpu.VMEM((2, 3, 3, 128, 128), BF16),
                pltpu.VMEM((2, 1792, 256), BF16),
                pltpu.VMEM((3, 3, 128, 256), BF16),
                pltpu.VMEM((3, 3, 256, 256), BF16),
                pltpu.VMEM((2, 2, 128), F32),
                pltpu.VMEM((2, 256), F32),
                pltpu.VMEM((1, 2, 256), F32),
                pltpu.VMEM((4, 8, 128), F32),
                pltpu.VMEM((4, GROUPS, 8, 128), F32),
                dma((ROWS,)), dma((15,)),
                dma((2,)), dma((2,)), dma((2,)), dma((2,)), dma((2,)), dma((2,)), dma((2,)), dma((2,)),
                dma((4, GROUPS)), dma((4, GROUPS)),
            ],
            compiler_params=pltpu.CompilerParams(
                collective_id=0, has_side_effects=True, vmem_limit_bytes=VLIM),
        )(images, w_a, norm_a, w_down, norm_down, w_b.reshape(3, 3, 256, 256), norm_b)
        return jnp.transpose(out.reshape(OROWS, OCOLS, NIM, 256), (2, 0, 1, 3))

    act_spec = P(('pod', 'dp'), 'sp', None, None)
    return jax.shard_map(local_stack, mesh=mesh, in_specs=(act_spec, P(), P(), P(), P(), P(), P()), out_specs=act_spec, check_vma=False)
```

time: 256 us -> 77 us (0.30)
  blocking collectives: 120 us -> 0 us
  Pallas kernels: 0 us -> 74.9 us
  matrix products: 66.9 us -> 0 us
  other arithmetic: 27 us -> 0 us
  waiting for transfers between devices: 17.7 us -> 0 us
  starting transfers between devices: 10.8 us -> 0 us
  local copies, waits for them, and re-layouts: 11.9 us -> 1.99 us
    psum x4 -> x0, blocking collectives: 120 us -> none  [batch_norm(): group_sums = lax.psum(local_sums, ('dp', 'sp'))]
    pallas_call x0 -> x1, Pallas kernels: none -> 74.9 us  [local_stack(): pl.pallas_call(kernel, out_shape=pltpu.VMEM((OROWS, OROW, 256), BF16), in...]
    conv_general_dilated x4 -> x0, matrix products: 66.9 us -> none  [the longest x3 59.2 us: same_layer(): lax.conv_general_dilated(padded, weight, (1, 1), ((0, 0), (1, 1)), dimens...]
    convert_element_type x4 -> x0, other arithmetic: 26.9 us -> none  [batch_norm(): return jnp.maximum(scaled, 0.0).astype(jnp.bfloat16)]
    ppermute x7 -> x0, waiting for transfers between devices: 17.7 us -> none  [the longest x3 14 us: same_layer(): bottom_rows = lax.ppermute(hidden[:, :1], 'sp', to_upper)]
    ppermute x7 -> x0, starting transfers between devices: 10.8 us -> none  [the longest x3 5.48 us: same_layer(): top_rows = lax.ppermute(hidden[:, -1:], 'sp', to_lower)]
    unnamed x13 -> x1, local copies, waits for them, and re-layouts: 9.86 us -> 1.99 us
  transfers between devices with their start and end apart: 7 -> 0, of which waited for: 7 -> 0; matrix products, arithmetic and copies ran while one was open for 0% -> 0% of each run, Pallas kernels for 0% -> 0%
where the time goes in v2:
time: 77 us; the launch traced here: 76.9 us
  Pallas kernels  74.9 us (97%)
  local copies, waits for them, and re-layouts  1.99 us (3%)
    pallas_call x1, Pallas kernels, local_stack(): pl.pallas_call(kernel, out_shape=pltpu.VMEM((OROWS, OROW, 256), BF16), in...  74.9 us
    unnamed x1, local copies, waits for them, and re-layouts  1.99 us

profile of v2, /device:TPU:0, one launch (start us, length us, event | category | flops | bytes accessed | tf_op | source)
XLA Modules:
  0.0 76.9 jit_solution(12947776706692678087)
XLA Ops:
  0.0 74.9 %shard_map.73 = bf16[6,1344,256]{2,1,0:T(8,128)(2,1)S(1)} custom-call(bf16[16,12,168,128]{3,2,1,0:T(8,128)(2,1)} %x_ref.1, bf16[2,3,3,128,128]{4,3,2,1,0:T(8,128)(2,1)} %wa_ref.1, f32[2,2,128]{2,1,0:T(2,128)} %na_ref.1, bf16[3,3,128,256]{3,2,1,0:T(8,128)(2,1)} %wd_ref.1, f32[2,256]{1,0:T(2,128)} %nd_ref.1, bf16[3,3,256,256]{3,2,1,0:T(8,128)(2,1)} %bitcast.5, ...), custom_call_target="tpu_custom_call" | custom-call | tf_op jit(solution)/shard_map/pallas_call | solution.py:439
  74.9 2.0 %copy.9 = bf16[16,6,84,256]{3,0,2,1:T(8,128)(2,1)} copy(bf16[16,6,84,256]{3,0,2,1:T(8,128)(2,1)S(1)} %bitcast.4) | data formatting | bytes 8257536

commit v3 on v2

--- a/solution.py
+++ b/solution.py
@@ -23,13 +23,14 @@
 OROW = OCOLS * NIM
 O3ROW = (OCOLS + 2) * NIM
 CHUNK = 336
-VLIM = 59 * 1024 * 1024
+NTR = 2
+VLIM = 60 * 1024 * 1024
 GROUPS = 8
 
 
 def kernel(x_ref, wa_ref, na_ref, wd_ref, nd_ref, wb_ref, nb_ref, out_ref,
-           xs, tr, yy, zz, y3, z3, wraw, wt, wdv, wbv, nav, ndv, nbv,
-           st_out, st_in,
+           xs, tr, yy, zz, y3, wraw, wt, wdv, wbv, nav, ndv, nbv,
+           cf, st_out, st_in,
            x_sem, w_sem, hx_send, hx_recv, h2_send, h2_recv, h3_send, h3_recv, h4_send, h4_recv,
            st_send, st_recv):
     dp = lax.axis_index("dp")
@@ -107,13 +108,16 @@
             yy[b, ROWS + 1] = jnp.zeros((YROW, 128), BF16)
         y3[OROWS + 1] = jnp.zeros((O3ROW, 256), BF16)
 
-    def transpose_row(r):
+    def transpose_piece(r, lo, hi, slot):
         for n in range(NIM):
-            tr[pl.ds(n * COLS, COLS), :] = xs[r, n].astype(F32)
-        for j in range(COLS):
-            v = tr[pl.ds(j, NIM, stride=COLS), :].astype(BF16)
+            tr[slot, pl.ds(n * COLS + lo, hi - lo), :] = xs[r, n, pl.ds(lo, hi - lo), :].astype(F32)
+        for j in range(lo, hi):
+            v = tr[slot, pl.ds(j, NIM, stride=COLS), :].astype(BF16)
             b, a = (j + 1) % 2, (j + 1) // 2
             yy[b, r, pl.ds(a * NIM, NIM), :] = v
+
+    def transpose_row(r):
+        transpose_piece(r, 0, COLS, 0)
 
     with jax.named_scope('transpose'):
         @pl.loop(0, 3)
@@ -190,9 +194,11 @@
     QUAD = ((0, 0), (1, 0), (0, NIM), (1, NIM))
 
     def pair_layer(layer, ahead, before):
-        def conv(i, carry):
+        def conv(i, carry, work=None):
             s1, s2 = carry
             for m in range(0, MROW, CHUNK):
+                if work is not None:
+                    work(i, m // CHUNK)
                 def take(taps, rows):
                     return jnp.concatenate(
                         [yy[plane, i + rr, pl.ds(m + off, CHUNK), :] for plane, off in taps for rr in rows], axis=1)
@@ -213,28 +219,22 @@
             i = 2 * it
             if before is not None:
                 before(it)
-            ahead(i)
-            return conv(i, carry)
-
-        def second(it, carry):
-            pair = jnp.where(it == 0, 4, (it - 1) * 5)
-
-            @pl.when(it == 1)
-            def _():
-                with jax.named_scope(f'near{layer}'):
-                    border_near(layer)
-
-            @pl.when(it == 2)
-            def _():
-                with jax.named_scope(f'far{layer}'):
-                    border_far(layer)
-            return conv(2 * pair, carry)
+            return conv(i, carry, ahead)
+
 
         zero = jnp.zeros((8, 128), F32)
         with jax.named_scope(f'pairA{layer}'):
-            carry = lax.fori_loop(1, 4, first, (zero, zero))
+            carry = (zero, zero)
+            for it in range(1, 4):
+                carry = first(it, carry)
+            carry = conv(8, carry)
         with jax.named_scope(f'pairB{layer}'):
-            s1, s2 = lax.fori_loop(0, 3, second, carry)
+            with jax.named_scope(f'near{layer}'):
+                border_near(layer)
+            carry = conv(0, carry)
+            with jax.named_scope(f'far{layer}'):
+                border_far(layer)
+            s1, s2 = conv(10, carry)
         total, finish = exchange(layer, [jnp.sum(s1, axis=0, keepdims=True), jnp.sum(s2, axis=0, keepdims=True)])
         mean, inv = moments(total[0:1], total[1:2], float(32 * 48 * 168))
         return mean, inv, finish
@@ -255,40 +255,53 @@
             else:
                 h2_far.wait_recv()
 
-    def norm_row(r, mean, inv, gamma, beta):
-        yy[1, r + 1, pl.ds(0, MROW), :] = normalise(zz[0, r], mean, inv, gamma, beta)
-        yy[0, r + 1, pl.ds(NIM, MROW), :] = normalise(zz[1, r], mean, inv, gamma, beta)
+    def norm_piece(r, m, size, coef):
+        par = load_coef(coef)
+        yy[1, r + 1, pl.ds(m, size), :] = normalise(zz[0, r, pl.ds(m, size), :], *par)
+        yy[0, r + 1, pl.ds(NIM + m, size), :] = normalise(zz[1, r, pl.ds(m, size), :], *par)
+
+    def norm_row(r, coef):
+        norm_piece(r, 0, MROW, coef)
+
+    def save_coef(slot, width, mean, inv, gamma, beta):
+        for k, v in enumerate((mean, inv, gamma, beta)):
+            cf[slot, k:k + 1, pl.ds(0, width)] = v
+        return slot
+
+    def load_coef(slot, lane=0):
+        return [cf[slot, k:k + 1, pl.ds(lane, 128)] for k in range(4)]
 
     def first_before(it):
+        if it == 1:
+            for r in range(6, ROWS):
+                x_copy(r).wait()
+
+    def first_ahead(i, c):
         for e in range(2):
-            x_copy(2 * it + 4 + e).wait()
-
-    def first_ahead(i):
-        transpose_row(i + 5)
-        transpose_row(i + 6)
+            transpose_piece(i + 5 + e, 48 * c, min(48 * c + 48, COLS), e % NTR)
 
     mean, inv, fin1 = pair_layer(0, first_ahead, first_before)
-    gamma, beta = nav[0, 0:1], nav[0, 1:2]
+    coef1 = save_coef(0, 128, mean, inv, nav[0, 0:1], nav[0, 1:2])
 
     with jax.named_scope('norm1'):
-        norm_row(ROWS - 1, mean, inv, gamma, beta)
+        norm_row(ROWS - 1, coef1)
 
         @pl.when(has_far)
         def _():
             h2_far.start()
-        norm_row(0, mean, inv, gamma, beta)
+        norm_row(0, coef1)
         h2_near.start()
 
         @pl.loop(1, 5)
         def _(r):
-            norm_row(r, mean, inv, gamma, beta)
-
-    def second_ahead(i):
-        norm_row(i + 3, mean, inv, gamma, beta)
-        norm_row(i + 4, mean, inv, gamma, beta)
+            norm_row(r, coef1)
+
+    def second_ahead(i, c):
+        for e in range(2):
+            norm_piece(i + 3 + e, c * CHUNK, CHUNK, coef1)
 
     mean2, inv2, fin2 = pair_layer(1, second_ahead, None)
-    gamma2, beta2 = nav[1, 0:1], nav[1, 1:2]
+    coef2 = save_coef(1, 128, mean2, inv2, nav[1, 0:1], nav[1, 1:2])
     h2_near.wait_send()
 
     @pl.when(has_far)
@@ -298,7 +311,7 @@
     sends_near = flip == 0
     sends_far = sp == 2
     with jax.named_scope('norm2'):
-        norm_row((ROWS - 1) * flip, mean2, inv2, gamma2, beta2)
+        norm_row((ROWS - 1) * flip, coef2)
 
         @pl.when(sends_near)
         def _():
@@ -310,16 +323,19 @@
 
         @pl.loop(1, ROWS)
         def _(r):
-            norm_row(r - flip, mean2, inv2, gamma2, beta2)
+            norm_row(r - flip, coef2)
 
     wd_taps = ((1, 0), (0, NIM), (1, NIM))
 
-    def wide_conv(i, lhs_of, w_val, carry):
+    def wide_conv(i, lhs_of, w_val, carry, work=None):
         s1, s2 = carry
         for m in range(0, OROW, CHUNK):
+            if work is not None:
+                work(m)
             lhs = jnp.concatenate(lhs_of(i, m), axis=1)
             res = jnp.dot(lhs, w_val, preferred_element_type=F32)
-            z3[i, pl.ds(m, CHUNK), :] = res
+            zz[0, i, pl.ds(m, CHUNK), :] = res[:, :128]
+            zz[1, i, pl.ds(m, CHUNK), :] = res[:, 128:]
             r3 = res.reshape(CHUNK // 8, 8, 256)
             s1 = s1 + jnp.sum(r3, axis=0)
             s2 = s2 + jnp.sum(r3 * r3, axis=0)
@@ -340,26 +356,31 @@
     def down_lhs(i, m):
         return [yy[plane, 2 * i - flip + p + 1, pl.ds(m + off, CHUNK), :] for p in range(3) for plane, off in wd_taps]
 
-    def down_body(it, carry):
-        @pl.when(it == OROWS - 1)
-        def _():
-            with jax.named_scope('halo2'):
-                @pl.when(flip == 1)
-                def _():
-                    h3_near.wait_recv()
-
-                @pl.when(sp == 1)
-                def _():
-                    h3_far.wait_recv()
-        return wide_conv(lax.rem(it + flip, OROWS), down_lhs, wdv[...].reshape(9 * 128, 256), carry)
-
+    wd_val = wdv[...].reshape(9 * 128, 256)
     with jax.named_scope('wide2'):
-        carry = lax.fori_loop(0, OROWS, down_body, (zero, zero))
+        carry = (zero, zero)
+        for it in range(OROWS - 1):
+            carry = wide_conv(it + flip, down_lhs, wd_val, carry)
+    with jax.named_scope('halo2'):
+        @pl.when(flip == 1)
+        def _():
+            h3_near.wait_recv()
+
+        @pl.when(sp == 1)
+        def _():
+            h3_far.wait_recv()
+    with jax.named_scope('wide2B'):
+        carry = wide_conv((OROWS - 1) * (1 - flip), down_lhs, wd_val, carry)
     mean3, inv3, fin3 = wide_stats(2, carry)
-    gamma3, beta3 = ndv[0:1], ndv[1:2]
+    coef3 = save_coef(2, 256, mean3, inv3, ndv[0:1], ndv[1:2])
+
+    def norm3_piece(r, m, size):
+        for h in range(2):
+            par = load_coef(coef3, 128 * h)
+            y3[r + 1, pl.ds(NIM + m, size), pl.ds(128 * h, 128)] = normalise(zz[h, r, pl.ds(m, size), :], *par)
 
     def norm3(r):
-        y3[r + 1, pl.ds(NIM, OROW), :] = normalise(z3[r], mean3, inv3, gamma3, beta3)
+        norm3_piece(r, 0, OROW)
 
     with jax.named_scope('norm3'):
         norm3(OROWS - 1)
@@ -380,36 +401,33 @@
     wb_val = wbv[...].reshape(9 * 256, 256)
 
     def last_first(it, carry):
-        norm3(it + 2)
-        return wide_conv(it, last_lhs, wb_val, carry)
-
-    def last_second(it, carry):
-        i = jnp.where(it < 2, it + 3, (it - 2) * 5)
-
-        @pl.when(it == 2)
-        def _():
-            with jax.named_scope('near3'):
-                h4_near.wait_recv()
-
-        @pl.when(it == 3)
-        def _():
-            with jax.named_scope('far3'):
-                @pl.when(has_far)
-                def _():
-                    h4_far.wait_recv()
-        return wide_conv(i, last_lhs, wb_val, carry)
+        return wide_conv(it, last_lhs, wb_val, carry, lambda m: norm3_piece(it + 2, m, CHUNK))
+
 
     with jax.named_scope('wide3A'):
-        carry = lax.fori_loop(1, 3, last_first, (zero, zero))
+        carry = (zero, zero)
+        for it in range(1, 3):
+            carry = last_first(it, carry)
     with jax.named_scope('wide3B'):
-        carry = lax.fori_loop(0, 4, last_second, carry)
+        for it in (3, 4):
+            carry = wide_conv(it, last_lhs, wb_val, carry)
+        with jax.named_scope('near3'):
+            h4_near.wait_recv()
+        carry = wide_conv(0, last_lhs, wb_val, carry)
+        with jax.named_scope('far3'):
+            @pl.when(has_far)
+            def _():
+                h4_far.wait_recv()
+        carry = wide_conv(OROWS - 1, last_lhs, wb_val, carry)
     mean4, inv4, fin4 = wide_stats(3, carry)
-    gamma4, beta4 = nbv[0, 0:1], nbv[0, 1:2]
+    coef4 = save_coef(3, 256, mean4, inv4, nbv[0, 0:1], nbv[0, 1:2])
 
     with jax.named_scope('out'):
         @pl.loop(0, OROWS)
         def _(r):
-            out_ref[r + flip * (OROWS - 1 - 2 * r)] = normalise(z3[r], mean4, inv4, gamma4, beta4)
+            for h in range(2):
+                out_ref[r + flip * (OROWS - 1 - 2 * r), :, pl.ds(128 * h, 128)] = normalise(
+                    zz[h, r], *load_coef(coef4, 128 * h))
 
     with jax.named_scope('drain'):
         hx_near.wait_send()
@@ -443,11 +461,10 @@
             out_specs=pl.BlockSpec(memory_space=pltpu.VMEM),
             scratch_shapes=[
                 pltpu.VMEM((ROWS + 2, NIM, COLS, 128), BF16),
-                pltpu.VMEM((NIM * COLS, 128), F32),
+                pltpu.VMEM((NTR, NIM * COLS, 128), F32),
                 pltpu.VMEM((2, ROWS + 2, YROW, 128), BF16),
                 pltpu.VMEM((2, ROWS, MROW, 128), F32),
                 pltpu.VMEM((OROWS + 2, O3ROW, 256), BF16),
-                pltpu.VMEM((OROWS, OROW, 256), F32),
                 pltpu.VMEM((2, 3, 3, 128, 128), BF16),
                 pltpu.VMEM((2, 1792, 256), BF16),
                 pltpu.VMEM((3, 3, 128, 256), BF16),
@@ -455,6 +472,7 @@
                 pltpu.VMEM((2, 2, 128), F32),
                 pltpu.VMEM((2, 256), F32),
                 pltpu.VMEM((1, 2, 256), F32),
+                pltpu.VMEM((4, 8, 256), F32),
                 pltpu.VMEM((4, 8, 128), F32),
                 pltpu.VMEM((4, GROUPS, 8, 128), F32),
                 dma((ROWS,)), dma((15,)),

time: 77 us -> 71.7 us (0.931)
  Pallas kernels: 74.9 us -> 69.6 us
    pallas_call x1, Pallas kernels: 74.9 us -> 69.6 us  [local_stack(): pl.pallas_call(kernel, out_shape=pltpu.VMEM((OROWS, OROW, 256), BF16), in...]
where the time goes in v3:
time: 71.7 us; the launch traced here: 71.6 us
  Pallas kernels  69.6 us (97%)
  local copies, waits for them, and re-layouts  1.99 us (3%)
    pallas_call x1, Pallas kernels, local_stack(): pl.pallas_call(kernel, out_shape=pltpu.VMEM((OROWS, OROW, 256), BF16), in...  69.6 us
    unnamed x1, local copies, waits for them, and re-layouts  1.99 us

profile of v3, /device:TPU:0, one launch (start us, length us, event | category | flops | bytes accessed | tf_op | source)
XLA Modules:
  0.0 71.6 jit_solution(15898402548164033694)
XLA Ops:
  0.0 69.6 %shard_map.73 = bf16[6,1344,256]{2,1,0:T(8,128)(2,1)S(1)} custom-call(bf16[16,12,168,128]{3,2,1,0:T(8,128)(2,1)} %x_ref.1, bf16[2,3,3,128,128]{4,3,2,1,0:T(8,128)(2,1)} %wa_ref.1, f32[2,2,128]{2,1,0:T(2,128)} %na_ref.1, bf16[3,3,128,256]{3,2,1,0:T(8,128)(2,1)} %wd_ref.1, f32[2,256]{1,0:T(2,128)} %nd_ref.1, bf16[3,3,256,256]{3,2,1,0:T(8,128)(2,1)} %bitcast.5, ...), custom_call_target="tpu_custom_call" | custom-call | tf_op jit(solution)/shard_map/pallas_call | solution.py:457
  69.6 2.0 %copy.9 = bf16[16,6,84,256]{3,0,2,1:T(8,128)(2,1)} copy(bf16[16,6,84,256]{3,0,2,1:T(8,128)(2,1)S(1)} %bitcast.4) | data formatting | bytes 8257536

commit v4 on v3

v4 whole, which is shorter than its diff:
```python
import functools

import jax
import jax.numpy as jnp
from jax import lax
from jax.experimental import pallas as pl
from jax.experimental.pallas import tpu as pltpu
from jax.sharding import PartitionSpec as P

EPS_VALUE = 1e-5
F32 = jnp.float32
BF16 = jnp.bfloat16
MESH = pl.DeviceIdType.MESH

NIM = 16
ROWS = 12
COLS = 168
HALF = COLS // 2
MROW = HALF * NIM
YROW = (HALF + 1) * NIM
OROWS = 6
OCOLS = 84
OROW = OCOLS * NIM
O3ROW = (OCOLS + 2) * NIM
CHUNK = 336
NTR = 2
VLIM = 56 * 1024 * 1024
GROUPS = 8
LANES = 128
WIDE = 256
LAST, FAR_SLOT = ROWS - 1, ROWS + 1
OLAST, OFAR = OROWS - 1, OROWS + 1
TWO_CHUNKS = 2 * CHUNK
SUB = CHUNK // 8
PIECES = range(0, MROW, CHUNK)


def head(size):
    return pl.ds(0, size)


def join(parts):
    return jnp.concatenate(parts, axis=1)


def mm(lhs, rhs):
    return jnp.dot(lhs, rhs, preferred_element_type=F32)


def sublane_sum(val):
    return jnp.sum(val, axis=0)


def column_sum(val):
    return jnp.sum(val, axis=0, keepdims=True)


def kernel(x_ref, wa_ref, na_ref, wd_ref, nd_ref, wb_ref, nb_ref, z_out, c_out,
           xs, tr, yy, zz, zo, y3, yx, ys, wx, wt, wdv, wbv, nav, ndv, nbv,
           cf, st_out, st_in, sw_out, sw_in,
           x_sem, w_sem, hx_send, hx_recv, h2_send, h2_recv, h3_send, h3_recv, h4_send, h4_recv,
           st_send, st_recv):
    dp = lax.axis_index("dp")
    sp = lax.axis_index("sp")
    me = dp * 4 + sp
    upright = lax.rem(sp, 2)
    flip = 1 - upright
    near = (0, dp, sp + 2 * flip - 1)
    far = (0, dp, lax.rem(7 - sp, 4))
    has_far = jnp.logical_or(sp == 1, sp == 2)

    def x_row(r):
        return r + flip * (LAST - 2 * r)

    def tap(p):
        return p + flip * (2 - 2 * p)

    def x_slot(r):
        return {9: 1, 10: 2, 11: 10, 0: 11}.get(r, r)

    def x_copy(r):
        return pltpu.make_async_copy(x_ref.at[:, x_row(r)], xs.at[x_slot(r)], x_sem.at[r])
    wa_copies = [pltpu.make_async_copy(wa_ref.at[l, tap(p)], ys.at[l, pl.ds(384 * p, 384)], w_sem.at[3 * l + p])
                 for l in range(2) for p in range(3)]
    w_copies = [pltpu.make_async_copy(na_ref, nav, w_sem.at[6]),
                pltpu.make_async_copy(nd_ref, ndv, w_sem.at[7]),
                pltpu.make_async_copy(nb_ref, nbv, w_sem.at[8])]
    for p in range(3):
        w_copies.append(pltpu.make_async_copy(wd_ref.at[tap(p)], wdv.at[p], w_sem.at[9 + p]))
        w_copies.append(pltpu.make_async_copy(wb_ref.at[tap(p)], wbv.at[p], w_sem.at[12 + p]))

    barrier = pltpu.get_barrier_semaphore()

    def peer(k):
        x, core = sp // 2, lax.rem(sp, 2)
        x = 1 - x if k & 2 else x
        core = 1 - core if k & 1 else core
        return (0, 1 - dp if k & 4 else dp, 2 * x + core)
    for k in range(1, GROUPS):
        pl.semaphore_signal(barrier, inc=1, device_id=peer(k), device_id_type=MESH)

    for r in (1, 2):
        x_copy(r).start()
    for c in wa_copies:
        c.start()
    for r in (3, 4, 5, 6, 7, 8, 11, 0):
        x_copy(r).start()
    for c in w_copies:
        c.start()

    def halo(src_near, dst_near, src_far, dst_far, send, recv):
        n_copy = pltpu.make_async_remote_copy(
            src_ref=src_near, dst_ref=dst_near, send_sem=send.at[0], recv_sem=recv.at[0],
            device_id=near, device_id_type=MESH)
        f_copy = pltpu.make_async_remote_copy(
            src_ref=src_far, dst_ref=dst_far, send_sem=send.at[1], recv_sem=recv.at[1],
            device_id=far, device_id_type=MESH)
        return n_copy, f_copy

    hx_near, hx_far = halo(x_ref.at[:, x_row(0)], xs.at[0], x_ref.at[:, x_row(LAST)], xs.at[9],
                           hx_send, hx_recv)
    h2_near, h2_far = halo(yy.at[:, 1], yy.at[:, 0], yy.at[:, ROWS], yy.at[:, FAR_SLOT], h2_send, h2_recv)
    h3_near, hy0 = halo(yy.at[:, 1], yy.at[:, FAR_SLOT], ys.at[0], yx.at[0], h3_send, h3_recv)
    hy1 = pltpu.make_async_remote_copy(
        src_ref=ys.at[1], dst_ref=yx.at[1], send_sem=h3_send.at[2], recv_sem=h3_recv.at[2],
        device_id=far, device_id_type=MESH)
    h4_near, h4_far = halo(y3.at[1], y3.at[0], y3.at[OROWS], y3.at[OFAR], h4_send, h4_recv)

    zpad = jnp.zeros((NIM, LANES), BF16)

    @pl.loop(0, ROWS + 2)
    def _(r):
        yy[0, r, head(NIM), :] = zpad
        yy[1, r, pl.ds(HALF * NIM, NIM), :] = zpad


    @pl.loop(0, OROWS + 2)
    def _(r):
        for c in (0, OCOLS + 1):
            y3[r, pl.ds(c * NIM, NIM), :] = jnp.zeros((NIM, WIDE), BF16)

    @pl.when(jnp.logical_not(has_far))
    def _():
        for b in range(2):
            yy[b, FAR_SLOT] = jnp.zeros((YROW, LANES), BF16)
        y3[OFAR] = jnp.zeros((O3ROW, WIDE), BF16)

    def transpose_piece(r, lo, hi, slot, src):
        for n in range(NIM):
            tr[slot, pl.ds(n * COLS + lo, hi - lo), :] = xs[src, n, pl.ds(lo, hi - lo), :].astype(F32)
        for j in range(lo, hi):
            v = tr[slot, pl.ds(j, NIM, stride=COLS), :].astype(BF16)
            b, a = (j + 1) % 2, (j + 1) // 2
            yy[b, r, pl.ds(a * NIM, NIM), :] = v

    def transpose_row(r, src):
        transpose_piece(r, 0, COLS, 0, src)

    with jax.named_scope('transpose'):
        @pl.loop(1, 3)
        def _(r):
            pltpu.make_async_copy(x_ref.at[:, x_row(r)], xs.at[r], x_sem.at[r]).wait()
            transpose_row(r + 1, r)
    for r in (9, 10):
        x_copy(r).start()

    with jax.named_scope('barrier'):
        pl.semaphore_wait(barrier, GROUPS - 1)

    @pl.when(has_far)
    def _():
        hx_far.start()
    hx_near.start()

    for c in wa_copies:
        c.wait()
    zblk = jnp.zeros((LANES, LANES), BF16)

    def tile(layer, p, q):
        return zblk if q is None else ys[layer, pl.ds(384 * p + LANES * q, LANES), :]

    for layer in range(2):
        def put(k, lo, hi):
            wt[layer, pl.ds(k, LANES), head(LANES)] = tile(layer, *lo)
            wt[layer, pl.ds(k, LANES), pl.ds(LANES, LANES)] = tile(layer, *hi)
        for q in range(3):
            put(WIDE * q, (1, q), (0, q))
            put(WIDE * q + LANES, (2, q), (1, q))
        for e, p in enumerate((0, 2)):
            k = 768 + 512 * e
            put(k, (p, 0), (p, None))
            put(k + LANES, (p, 1), (p, 0))
            put(k + WIDE, (p, 2), (p, 1))
            put(k + 384, (p, None), (p, 2))
    for k, (lo, hi) in enumerate(((0, None), (1, 0), (2, 1), (None, 2))):
        wx[pl.ds(LANES * k, LANES), head(LANES)] = tile(1, 1, lo)
        wx[pl.ds(LANES * k, LANES), pl.ds(LANES, LANES)] = tile(1, 1, hi)

    ys[0, head(NIM), :] = zpad
    ys[1, pl.ds(HALF * NIM, NIM), :] = zpad

    with jax.named_scope('transpose2'):
        @pl.loop(3, 5)
        def _(r):
            pltpu.make_async_copy(x_ref.at[:, x_row(r)], xs.at[r], x_sem.at[r]).wait()
            transpose_row(r + 1, r)
    for r in (5, 6, 7, 8, 11, 0, 9, 10):
        x_copy(r).wait()
    for c in w_copies:
        c.wait()

    def exchange(layer, rows, meanwhile=None):
        out, slots = (st_out, st_in) if layer < 2 else (sw_out, sw_in)
        at = layer % 2
        buf = join(rows)
        out[at] = buf
        slots[at, me] = buf
        copies = []
        for k in (7, 6, 5, 4, 3, 2, 1):
            copies.append(pltpu.make_async_remote_copy(
                src_ref=out.at[at], dst_ref=slots.at[at, me],
                send_sem=st_send.at[layer, k], recv_sem=st_recv.at[layer, k],
                device_id=peer(k), device_id_type=MESH))
        for c in copies:
            c.start()
        if meanwhile is not None:
            meanwhile()
        with jax.named_scope(f'stat{layer}'):
            for c in copies:
                c.wait_recv()
        total = slots[at, 0]
        for s in range(1, GROUPS):
            total = total + slots[at, s]

        def finish():
            for c in copies:
                c.wait_send()
        half = total.shape[1] // 2
        return total[:, :half], total[:, half:], finish

    def moments(s1, s2, count):
        mean = s1 / count
        var = s2 / count - mean * mean
        return mean, lax.rsqrt(var + EPS_VALUE)

    def normalise(z, mean, inv, gamma, beta):
        return jnp.maximum(gamma * (z - mean) * inv + beta, 0.0).astype(BF16)

    TAPS = (((0, 0), (1, 0), (0, NIM)), ((1, 0), (0, NIM), (1, NIM)))
    QUAD = ((0, 0), (1, 0), (0, NIM), (1, NIM))

    def pair_layer(layer, ahead, near_row, far_row, meanwhile=None):
        def conv(i, carry, work=None):
            s1, s2 = carry
            for m in PIECES:
                if work is not None:
                    work(i, m // CHUNK)
                def take(taps, rows):
                    return join(
                        [yy[plane, i + rr, pl.ds(m + off, CHUNK), :] for plane, off in taps for rr in rows])
                mid = [mm(take(TAPS[b], (1, 2)), wt[layer, head(768), :])
                       for b in range(2)]
                edge = [mm(take(QUAD, (3 * e,)), wt[layer, pl.ds(768 + 512 * e, 512), :]) for e in range(2)]
                for b in range(2):
                    for e in range(2):
                        z = mid[b][:, LANES * e:LANES * e + LANES] + edge[e][:, LANES * b:LANES * b + LANES]
                        zz[b, i + e, pl.ds(m, CHUNK), :] = z
                        z8 = z.reshape(SUB, 8, LANES)
                        s1 = s1 + sublane_sum(z8)
                        s2 = s2 + sublane_sum(z8 * z8)
            return s1, s2

        def border(it, carry):
            @pl.when(it == 0)
            def _():
                near_row.wait_recv()

            @pl.when(jnp.logical_and(it == 1, has_far))
            def _():
                far_row.wait_recv()
            if layer == 0:
                @pl.when(jnp.logical_or(it == 0, has_far))
                def _():
                    transpose_row(it * (FAR_SLOT), it * 9)
            return conv(10 * it, carry)

        zero = jnp.zeros((8, LANES), F32)
        carry = (zero, zero)
        with jax.named_scope(f'pairA{layer}'):
            for i in (2, 4, 6, 8):
                carry = conv(i, carry, ahead)
        if layer == 1:
            @pl.when(sp == 2)
            def _():
                hy0.start()
        with jax.named_scope(f'pairB{layer}'):
            s1, s2 = lax.fori_loop(0, 2, border, carry)
        s1, s2, finish = exchange(layer, [column_sum(s1), column_sum(s2)],
                                  meanwhile)
        mean, inv = moments(s1, s2, float(32 * 48 * 168))
        return mean, inv, finish

    def norm_piece(r, m, size, coef, slot=None, copy_too=False):
        par = load_coef(coef)
        slot = r + 1 if slot is None else slot
        for b, plane, off in ((0, 1, m), (1, 0, NIM + m)):
            val = normalise(zz[b, r, pl.ds(m, size), :], *par)
            yy[plane, slot, pl.ds(off, size), :] = val
            if copy_too:
                ys[plane, pl.ds(off, size), :] = val

    def norm_row(r, coef):
        norm_piece(r, 0, MROW, coef)

    def save_coef(slot, width, mean, inv, gamma, beta):
        for k, v in enumerate((mean, inv, gamma, beta)):
            cf[slot, k:k + 1, head(width)] = v
        return slot

    def load_coef(slot, lane=0):
        return [cf[slot, k:k + 1, pl.ds(lane, LANES)] for k in range(4)]

    def first_ahead(i, c):
        for e in range(2):
            r = i + 3 + e if i < 8 else (LAST) * (1 - e)
            transpose_piece(r + 1, 48 * c, min(48 * c + 48, COLS), e % NTR, x_slot(r))

    mean, inv, fin1 = pair_layer(0, first_ahead, hx_near, hx_far)
    coef1 = save_coef(0, LANES, mean, inv, nav[0, 0:1], nav[0, 1:2])

    with jax.named_scope('norm1'):
        norm_row(LAST, coef1)

        @pl.when(has_far)
        def _():
            h2_far.start()
        norm_row(0, coef1)
        h2_near.start()

        @pl.loop(1, 5)
        def _(r):
            norm_piece(r, 0, TWO_CHUNKS, coef1)

    def second_ahead(i, c):
        if i == 2 and c < 2:
            for r in range(1, 5):
                norm_piece(r, (c + 2) * CHUNK, CHUNK, coef1)
        if i < 8:
            for r in (i + 3, i + 4):
                if r < LAST:
                    norm_piece(r, c * CHUNK, CHUNK, coef1, None, r == ROWS - 2)

    def lone_row(m, taps):
        res = None
        for p in taps:
            src = (yy.at[:, ROWS], yy.at[:, FAR_SLOT], yx)[p]
            lhs = join([src[plane, pl.ds(m + off, CHUNK), :] for plane, off in QUAD])
            w_val = wx[...] if p == 1 else wt[1, pl.ds(768 + WIDE * p, 512), :]
            part = mm(lhs, w_val)
            res = part if res is None else res + part
        return res

    def second_meanwhile():
        @pl.when(sp == 2)
        def _():
            hy1.start()

        @pl.when(sp == 1)
        def _():
            for m in PIECES:
                res = lone_row(m, (0, 1))
                tr[0, pl.ds(m, CHUNK), :] = res[:, :LANES]
                tr[1, pl.ds(m, CHUNK), :] = res[:, LANES:]

    mean2, inv2, fin2 = pair_layer(1, second_ahead, h2_near, h2_far, second_meanwhile)
    coef2 = save_coef(1, LANES, mean2, inv2, nav[1, 0:1], nav[1, 1:2])
    h2_near.wait_send()

    @pl.when(has_far)
    def _():
        h2_far.wait_send()

    sends_near = upright == 1
    with jax.named_scope('norm2'):
        norm_piece(flip, 0, MROW, coef2, 1)

        @pl.when(sends_near)
        def _():
            h3_near.start()
        for r in (1, 2):
            norm_piece(r + flip, 0, TWO_CHUNKS, coef2, r + 1)

    wd_taps = ((1, 0), (0, NIM), (1, NIM))

    def wide_conv(dst, i, lhs_of, w_val, carry, work=None):
        s1, s2 = carry
        for m in PIECES:
            if work is not None:
                work(m)
            lhs = join(lhs_of(m))
            res = mm(lhs, w_val)
            dst[0, i, pl.ds(m, CHUNK), :] = res[:, :LANES]
            dst[1, i, pl.ds(m, CHUNK), :] = res[:, LANES:]
            r3 = res.reshape(SUB, 8, WIDE)
            s1 = s1 + sublane_sum(r3)
            s2 = s2 + sublane_sum(r3 * r3)
        return s1, s2

    def wide_stats(layer, carry):
        s1, s2 = carry
        s1, s2, finish = exchange(layer, [column_sum(s1), column_sum(s2)])
        mean, inv = moments(s1, s2, float(32 * 24 * 84))
        return mean, inv, finish

    zero = jnp.zeros((8, WIDE), F32)

    def down_lhs(slots):
        return lambda m: [yy[plane, slot, pl.ds(m + off, CHUNK), :] for slot in slots for plane, off in wd_taps]

    wd_val = wdv[...].reshape(9 * LANES, WIDE)

    def down_ahead(it):
        def work(m):
            if it == 0 and m < TWO_CHUNKS:
                for r in (1, 2):
                    norm_piece(r + flip, m + TWO_CHUNKS, CHUNK, coef2, r + 1)
            for e in range(2):
                norm_piece(2 * it + 3 + e + flip, m, CHUNK, coef2, 2 * it + 4 + e)
        return work if it < 4 else None

    with jax.named_scope('wide2'):
        carry = (zero, zero)
        for it in range(OLAST):
            carry = wide_conv(zo, it, down_lhs((2 * it + 1, 2 * it + 2, 2 * it + 3)), wd_val, carry, down_ahead(it))

    with jax.named_scope('halo2'):
        @pl.when(sp == 1)
        def _():
            hy0.wait_recv()
            hy1.wait_recv()

            par = load_coef(coef2)
            for m in PIECES:
                res = lone_row(m, (2,))
                for b, plane, off in ((0, 1, m), (1, 0, NIM + m)):
                    z = tr[b, pl.ds(m, CHUNK), :] + res[:, LANES * b:LANES * b + LANES]
                    yy[plane, FAR_SLOT, pl.ds(off, CHUNK), :] = normalise(z, *par)

        norm_piece((LAST) * upright, 0, MROW, coef2, ROWS * upright)

        @pl.when(flip == 1)
        def _():
            h3_near.wait_recv()
    with jax.named_scope('wide2B'):
        slots = (LAST + 2 * flip, ROWS * upright, FAR_SLOT - ROWS * flip)
        carry = wide_conv(zo, OLAST, down_lhs(slots), wd_val, carry)
    mean3, inv3, fin3 = wide_stats(2, carry)
    coef3 = save_coef(2, WIDE, mean3, inv3, ndv[0:1], ndv[1:2])

    def norm3_piece(r, m, size):
        step = lax.rem(r - flip + OROWS, OROWS)
        for h in range(2):
            par = load_coef(coef3, LANES * h)
            y3[r + 1, pl.ds(NIM + m, size), pl.ds(LANES * h, LANES)] = normalise(zo[h, step, pl.ds(m, size), :], *par)

    def norm3(r):
        norm3_piece(r, 0, OROW)

    with jax.named_scope('norm3'):
        norm3(OLAST)

        @pl.when(has_far)
        def _():
            h4_far.start()

        norm3(0)
        h4_near.start()

        @pl.loop(1, 3)
        def _(r):
            norm3_piece(r, 0, TWO_CHUNKS)

    def last_lhs(i, taps=(0, 1, 2)):
        return lambda m: [y3[i + p, pl.ds(m + NIM * q, CHUNK), :] for p in taps for q in range(3)]

    wb_val = wbv[...].reshape(9 * WIDE, WIDE)

    def last_ahead(it):
        def work(m):
            if it == 1:
                if m < TWO_CHUNKS:
                    for r in range(1, 3):
                        norm3_piece(r, m + TWO_CHUNKS, CHUNK)
                norm3_piece(3, m, CHUNK)
            elif it == 2:
                norm3_piece(4, m, CHUNK)
        return work

    with jax.named_scope('wide3A'):
        carry = (zero, zero)
        for it in (1, 2, 3, 4):
            carry = wide_conv(z_out, it, last_lhs(it), wb_val, carry, last_ahead(it))
    with jax.named_scope('wide3B'):
        with jax.named_scope('near3'):
            h4_near.wait_recv()
        carry = wide_conv(z_out, 0, last_lhs(0), wb_val, carry)
        part_w = wbv[head(2)].reshape(6 * WIDE, WIDE)
        last_w = wbv[2].reshape(3 * WIDE, WIDE)
        r = OLAST
        for m in PIECES:
            res = mm(join(last_lhs(r, (0, 1))(m)), part_w)
            z_out[0, r, pl.ds(m, CHUNK), :] = res[:, :LANES]
            z_out[1, r, pl.ds(m, CHUNK), :] = res[:, LANES:]
        with jax.named_scope('far3'):
            @pl.when(has_far)
            def _():
                h4_far.wait_recv()
        s1, s2 = carry
        for m in PIECES:
            res = mm(join(last_lhs(r, (2,))(m)), last_w)
            res = res + join([z_out[h, r, pl.ds(m, CHUNK), :] for h in range(2)])
            z_out[0, r, pl.ds(m, CHUNK), :] = res[:, :LANES]
            z_out[1, r, pl.ds(m, CHUNK), :] = res[:, LANES:]
            r3 = res.reshape(SUB, 8, WIDE)
            s1 = s1 + sublane_sum(r3)
            s2 = s2 + sublane_sum(r3 * r3)
        carry = s1, s2
    mean4, inv4, fin4 = wide_stats(3, carry)
    for k, v in enumerate((mean4, inv4, nbv[0, 0:1], nbv[0, 1:2])):
        c_out[k:k + 1] = v

    with jax.named_scope('drain'):
        hx_near.wait_send()
        h4_near.wait_send()

        @pl.when(has_far)
        def _():
            hx_far.wait_send()
            h4_far.wait_send()

        @pl.when(sends_near)
        def _():
            h3_near.wait_send()

        @pl.when(sp == 2)
        def _():
            hy0.wait_send()
            hy1.wait_send()
        for f in (fin1, fin2, fin3, fin4):
            f()


def result_kernel(z_ref, c_ref, out_ref, yo, cf, sem):
    flip = 1 - lax.rem(lax.axis_index("sp"), 2)

    def copy(r):
        return pltpu.make_async_copy(yo.at[r], out_ref.at[r + flip * (OLAST - 2 * r)], sem.at[r])

    mean, inv, gamma, beta = [c_ref[k:k + 1] for k in range(4)]
    scale = gamma * inv
    cf[0:1] = scale
    cf[1:2] = beta - mean * scale
    small = jnp.logical_and(jnp.max(jnp.abs(scale)) < 1e15, jnp.max(jnp.abs(mean)) < 1e20)

    @pl.when(small)
    def _():
        @pl.loop(0, OROWS)
        def _(r):
            for h in range(2):
                lanes = pl.ds(LANES * h, LANES)
                y = z_ref[h, r] * cf[0:1, lanes] + cf[1:2, lanes]
                yo[r, :, lanes] = jnp.maximum(y, 0.0).astype(BF16)
            copy(r).start()

    @pl.when(jnp.logical_not(small))
    def _():
        @pl.loop(0, OROWS)
        def _(r):
            for h in range(2):
                lanes = pl.ds(LANES * h, LANES)
                mean, inv, gamma, beta = [c_ref[k:k + 1, lanes] for k in range(4)]
                yo[r, :, lanes] = jnp.maximum(gamma * (z_ref[h, r] - mean) * inv + beta, 0.0).astype(BF16)
            copy(r).start()

    @pl.loop(0, OROWS)
    def _(r):
        copy(r).wait()


def solution(mesh):
    any_spec = pl.BlockSpec(memory_space=pl.ANY)
    dma = pltpu.SemaphoreType.DMA

    def local_stack(images, w_a, norm_a, w_down, norm_down, w_b, norm_b):
        z_last, coef = pl.pallas_call(
            kernel,
            out_shape=(pltpu.VMEM((2, OROWS, OROW, LANES), F32), pltpu.VMEM((8, WIDE), F32)),
            in_specs=[any_spec] * 7,
            out_specs=(pl.BlockSpec(memory_space=pltpu.VMEM),) * 2,
            scratch_shapes=[
                pltpu.VMEM((12, NIM, COLS, LANES), BF16),
                pltpu.VMEM((NTR, NIM * COLS, LANES), F32),
                pltpu.VMEM((2, ROWS + 2, YROW, LANES), BF16),
                pltpu.VMEM((2, ROWS, MROW, LANES), F32),
                pltpu.VMEM((2, OROWS, OROW, LANES), F32),
                pltpu.VMEM((OROWS + 2, O3ROW, WIDE), BF16),
                pltpu.VMEM((2, YROW, LANES), BF16),
                pltpu.VMEM((2, YROW, LANES), BF16),
                pltpu.VMEM((512, WIDE), BF16),
                pltpu.VMEM((2, 1792, WIDE), BF16),
                pltpu.VMEM((3, 3, LANES, WIDE), BF16),
                pltpu.VMEM((3, 3, WIDE, WIDE), BF16),
                pltpu.VMEM((2, 2, LANES), F32),
                pltpu.VMEM((2, WIDE), F32),
                pltpu.VMEM((1, 2, WIDE), F32),
                pltpu.VMEM((4, 8, WIDE), F32),
                pltpu.VMEM((2, 1, WIDE), F32),
                pltpu.VMEM((2, GROUPS, 1, WIDE), F32),
                pltpu.VMEM((2, 1, 512), F32),
                pltpu.VMEM((2, GROUPS, 1, 512), F32),
                dma((ROWS,)), dma((15,)),
                *[dma((2,))] * 4, *[dma((3,))] * 2, *[dma((2,))] * 2,
                *[dma((4, GROUPS))] * 2,
            ],
            compiler_params=pltpu.CompilerParams(
                collective_id=0, has_side_effects=True, vmem_limit_bytes=VLIM),
        )(images, w_a.reshape(2, 3, 384, LANES), norm_a, w_down, norm_down, w_b.reshape(3, 3, WIDE, WIDE), norm_b)
        out = pl.pallas_call(
            result_kernel,
            out_shape=jax.ShapeDtypeStruct((OROWS, OROW, WIDE), BF16),
            in_specs=[pl.BlockSpec(memory_space=pltpu.VMEM)] * 2,
            out_specs=any_spec,
            scratch_shapes=[pltpu.VMEM((OROWS, OROW, WIDE), BF16), pltpu.VMEM((8, WIDE), F32), dma((OROWS,))],
            compiler_params=pltpu.CompilerParams(vmem_limit_bytes=6 * 1024 * 1024),
        )(z_last, coef)
        return jnp.transpose(out.reshape(OROWS, OCOLS, NIM, WIDE), (2, 0, 1, 3))

    act_spec = P(('pod', 'dp'), 'sp', None, None)
    return jax.shard_map(local_stack, mesh=mesh, in_specs=(act_spec, P(), P(), P(), P(), P(), P()), out_specs=act_spec, check_vma=False)
```

time: 71.7 us -> 66.2 us (0.923)
  Pallas kernels: 69.6 us -> 65.9 us
  local copies, waits for them, and re-layouts: 1.99 us -> 0 us
    pallas_call x1 -> x2, Pallas kernels: 69.6 us -> 65.9 us  [the longest x1 63.6 us: local_stack(): pl.pallas_call(kernel, out_shape=(pltpu.VMEM((2, OROWS, OROW, LANES), F32...]
    unnamed x1 -> x0, local copies, waits for them, and re-layouts: 1.99 us -> none
where the time goes in v4:
time: 66.2 us; the launch traced here: 66.1 us
  Pallas kernels  65.9 us (100%)
    pallas_call x1, Pallas kernels, local_stack(): pl.pallas_call(kernel, out_shape=(pltpu.VMEM((2, OROWS, OROW, LANES), F32...  63.6 us
    pallas_call x1, Pallas kernels, local_stack(): pl.pallas_call(result_kernel, out_shape=jax.ShapeDtypeStruct((OROWS, OROW...  2.36 us

profile of v4, /device:TPU:0, one launch (start us, length us, event | category | flops | bytes accessed | tf_op | source)
XLA Modules:
  0.0 66.1 jit_solution(9564596851648423304)
XLA Ops:
  0.0 63.6 %shard_map.73 = (f32[2,6,1344,128]{3,2,1,0:T(8,128)S(1)}, f32[8,256]{1,0:T(8,128)S(1)}) custom-call(bf16[16,12,168,128]{3,2,1,0:T(8,128)(2,1)} %x_ref.1, bf16[2,3,384,128]{3,2,1,0:T(8,128)(2,1)} %bitcast.6, f32[2,2,128]{2,1,0:T(2,128)} %na_ref.1, bf16[3,3,128,256]{3,2,1,0:T(8,128)(2,1)} %wd_ref.1, f32[2,256]{1,0:T(2,128)} %nd_ref.1, ...), custom_call_target="tpu_custom_call" | custom-call | tf_op jit(solution)/shard_map/pallas_call | solution.py:595
  63.6 2.4 %shard_map.74 = bf16[6,1344,256]{2,1,0:T(8,128)(2,1)} custom-call(f32[2,6,1344,128]{3,2,1,0:T(8,128)S(1)} %get-tuple-element.7.z_ref, f32[8,256]{1,0:T(8,128)S(1)} %get-tuple-element.8.c_ref), custom_call_target="tpu_custom_call" | custom-call | tf_op jit(solution)/shard_map/pallas_call | solution.py:628

commit v5 on v4

--- a/solution.py
+++ b/solution.py
@@ -30,9 +30,14 @@
 WIDE = 256
 LAST, FAR_SLOT = ROWS - 1, ROWS + 1
 OLAST, OFAR = OROWS - 1, OROWS + 1
-TWO_CHUNKS = 2 * CHUNK
+FIRST = CHUNK + NIM
 SUB = CHUNK // 8
 PIECES = range(0, MROW, CHUNK)
+
+
+def rest(m):
+    lo = min(FIRST + m, MROW)
+    return lo, min(CHUNK, MROW - lo)
 
 
 def head(size):
@@ -105,8 +110,6 @@
         c.start()
     for r in (3, 4, 5, 6, 7, 8, 11, 0):
         x_copy(r).start()
-    for c in w_copies:
-        c.start()
 
     def halo(src_near, dst_near, src_far, dst_far, send, recv):
         n_copy = pltpu.make_async_remote_copy(
@@ -207,7 +210,7 @@
     for r in (5, 6, 7, 8, 11, 0, 9, 10):
         x_copy(r).wait()
     for c in w_copies:
-        c.wait()
+        c.start()
 
     def exchange(layer, rows, meanwhile=None):
         out, slots = (st_out, st_in) if layer < 2 else (sw_out, sw_in)
@@ -301,6 +304,8 @@
         return mean, inv, finish
 
     def norm_piece(r, m, size, coef, slot=None, copy_too=False):
+        if size == 0:
+            return
         par = load_coef(coef)
         slot = r + 1 if slot is None else slot
         for b, plane, off in ((0, 1, m), (1, 0, NIM + m)):
@@ -326,6 +331,8 @@
             transpose_piece(r + 1, 48 * c, min(48 * c + 48, COLS), e % NTR, x_slot(r))
 
     mean, inv, fin1 = pair_layer(0, first_ahead, hx_near, hx_far)
+    for c in w_copies:
+        c.wait()
     coef1 = save_coef(0, LANES, mean, inv, nav[0, 0:1], nav[0, 1:2])
 
     with jax.named_scope('norm1'):
@@ -339,12 +346,12 @@
 
         @pl.loop(1, 5)
         def _(r):
-            norm_piece(r, 0, TWO_CHUNKS, coef1)
+            norm_piece(r, 0, FIRST, coef1)
 
     def second_ahead(i, c):
-        if i == 2 and c < 2:
+        if i == 2:
             for r in range(1, 5):
-                norm_piece(r, (c + 2) * CHUNK, CHUNK, coef1)
+                norm_piece(r, *rest(c * CHUNK), coef1)
         if i < 8:
             for r in (i + 3, i + 4):
                 if r < LAST:
@@ -388,7 +395,7 @@
         def _():
             h3_near.start()
         for r in (1, 2):
-            norm_piece(r + flip, 0, TWO_CHUNKS, coef2, r + 1)
+            norm_piece(r + flip, 0, FIRST, coef2, r + 1)
 
     wd_taps = ((1, 0), (0, NIM), (1, NIM))
 
@@ -421,12 +428,15 @@
 
     def down_ahead(it):
         def work(m):
-            if it == 0 and m < TWO_CHUNKS:
+            if it == 0:
                 for r in (1, 2):
-                    norm_piece(r + flip, m + TWO_CHUNKS, CHUNK, coef2, r + 1)
-            for e in range(2):
-                norm_piece(2 * it + 3 + e + flip, m, CHUNK, coef2, 2 * it + 4 + e)
-        return work if it < 4 else None
+                    norm_piece(r + flip, *rest(m), coef2, r + 1)
+            if it < 4:
+                for e in range(2):
+                    norm_piece(2 * it + 3 + e + flip, m, CHUNK, coef2, 2 * it + 4 + e)
+            else:
+                norm_piece(LAST * upright, m, CHUNK, coef2, ROWS)
+        return work
 
     with jax.named_scope('wide2'):
         carry = (zero, zero)
@@ -446,18 +456,19 @@
                     z = tr[b, pl.ds(m, CHUNK), :] + res[:, LANES * b:LANES * b + LANES]
                     yy[plane, FAR_SLOT, pl.ds(off, CHUNK), :] = normalise(z, *par)
 
-        norm_piece((LAST) * upright, 0, MROW, coef2, ROWS * upright)
 
         @pl.when(flip == 1)
         def _():
             h3_near.wait_recv()
     with jax.named_scope('wide2B'):
-        slots = (LAST + 2 * flip, ROWS * upright, FAR_SLOT - ROWS * flip)
+        slots = (LAST + 2 * flip, ROWS, FAR_SLOT - ROWS * flip)
         carry = wide_conv(zo, OLAST, down_lhs(slots), wd_val, carry)
     mean3, inv3, fin3 = wide_stats(2, carry)
     coef3 = save_coef(2, WIDE, mean3, inv3, ndv[0:1], ndv[1:2])
 
     def norm3_piece(r, m, size):
+        if size == 0:
+            return
         step = lax.rem(r - flip + OROWS, OROWS)
         for h in range(2):
             par = load_coef(coef3, LANES * h)
@@ -478,7 +489,7 @@
 
         @pl.loop(1, 3)
         def _(r):
-            norm3_piece(r, 0, TWO_CHUNKS)
+            norm3_piece(r, 0, FIRST)
 
     def last_lhs(i, taps=(0, 1, 2)):
         return lambda m: [y3[i + p, pl.ds(m + NIM * q, CHUNK), :] for p in taps for q in range(3)]
@@ -488,9 +499,8 @@
     def last_ahead(it):
         def work(m):
             if it == 1:
-                if m < TWO_CHUNKS:
-                    for r in range(1, 3):
-                        norm3_piece(r, m + TWO_CHUNKS, CHUNK)
+                for r in range(1, 3):
+                    norm3_piece(r, *rest(m))
                 norm3_piece(3, m, CHUNK)
             elif it == 2:
                 norm3_piece(4, m, CHUNK)

time: 66.2 us -> 65.2 us (0.985)
  Pallas kernels: 65.9 us -> 64.9 us
    pallas_call x1, Pallas kernels: 63.6 us -> 62.6 us  [local_stack(): pl.pallas_call(kernel, out_shape=(pltpu.VMEM((2, OROWS, OROW, LANES), F32...]
where the time goes in v5:
time: 65.2 us; the launch traced here: 65.1 us
  Pallas kernels  64.9 us (100%)
    pallas_call x1, Pallas kernels, local_stack(): pl.pallas_call(kernel, out_shape=(pltpu.VMEM((2, OROWS, OROW, LANES), F32...  62.6 us
    pallas_call x1, Pallas kernels, local_stack(): pl.pallas_call(result_kernel, out_shape=jax.ShapeDtypeStruct((OROWS, OROW...  2.36 us

profile of v5, /device:TPU:0, one launch (start us, length us, event | category | flops | bytes accessed | tf_op | source)
XLA Modules:
  0.0 65.1 jit_solution(13294936878196105144)
XLA Ops:
  0.0 62.6 %shard_map.73 = (f32[2,6,1344,128]{3,2,1,0:T(8,128)S(1)}, f32[8,256]{1,0:T(8,128)S(1)}) custom-call(bf16[16,12,168,128]{3,2,1,0:T(8,128)(2,1)} %x_ref.1, bf16[2,3,384,128]{3,2,1,0:T(8,128)(2,1)} %bitcast.6, f32[2,2,128]{2,1,0:T(2,128)} %na_ref.1, bf16[3,3,128,256]{3,2,1,0:T(8,128)(2,1)} %wd_ref.1, f32[2,256]{1,0:T(2,128)} %nd_ref.1, ...), custom_call_target="tpu_custom_call" | custom-call | tf_op jit(solution)/shard_map/pallas_call | solution.py:605
  62.6 2.4 %shard_map.74 = bf16[6,1344,256]{2,1,0:T(8,128)(2,1)} custom-call(f32[2,6,1344,128]{3,2,1,0:T(8,128)S(1)} %get-tuple-element.7.z_ref, f32[8,256]{1,0:T(8,128)S(1)} %get-tuple-element.8.c_ref), custom_call_target="tpu_custom_call" | custom-call | tf_op jit(solution)/shard_map/pallas_call | solution.py:638

commit v6 on v5

--- a/solution.py
+++ b/solution.py
@@ -61,7 +61,7 @@
 
 
 def kernel(x_ref, wa_ref, na_ref, wd_ref, nd_ref, wb_ref, nb_ref, z_out, c_out,
-           xs, tr, yy, zz, zo, y3, yx, ys, wx, wt, wdv, wbv, nav, ndv, nbv,
+           xs, yy, zz, zo, y3, yx, ys, wx, wt, wdv, wbv, nav, ndv, nbv,
            cf, st_out, st_in, sw_out, sw_in,
            x_sem, w_sem, hx_send, hx_recv, h2_send, h2_recv, h3_send, h3_recv, h4_send, h4_recv,
            st_send, st_recv):
@@ -144,15 +144,14 @@
 
     @pl.when(jnp.logical_not(has_far))
     def _():
-        for b in range(2):
-            yy[b, FAR_SLOT] = jnp.zeros((YROW, LANES), BF16)
+        xs[9] = jnp.zeros((NIM, COLS, LANES), BF16)
         y3[OFAR] = jnp.zeros((O3ROW, WIDE), BF16)
 
     def transpose_piece(r, lo, hi, slot, src):
         for n in range(NIM):
-            tr[slot, pl.ds(n * COLS + lo, hi - lo), :] = xs[src, n, pl.ds(lo, hi - lo), :].astype(F32)
+            zo[slot, pl.ds(n * COLS + lo, hi - lo), :] = xs[src, n, pl.ds(lo, hi - lo), :].astype(F32)
         for j in range(lo, hi):
-            v = tr[slot, pl.ds(j, NIM, stride=COLS), :].astype(BF16)
+            v = zo[slot, pl.ds(j, NIM, stride=COLS), :].astype(BF16)
             b, a = (j + 1) % 2, (j + 1) // 2
             yy[b, r, pl.ds(a * NIM, NIM), :] = v
 
@@ -281,11 +280,10 @@
             @pl.when(jnp.logical_and(it == 1, has_far))
             def _():
                 far_row.wait_recv()
-            if layer == 0:
-                @pl.when(jnp.logical_or(it == 0, has_far))
-                def _():
-                    transpose_row(it * (FAR_SLOT), it * 9)
-            return conv(10 * it, carry)
+
+            def halo_ahead(i, c):
+                transpose_piece(it * FAR_SLOT, 48 * c, min(48 * c + 48, COLS), c % NTR, it * 9)
+            return conv(10 * it, carry, halo_ahead if layer == 0 else None)
 
         zero = jnp.zeros((8, LANES), F32)
         carry = (zero, zero)
@@ -376,8 +374,8 @@
         def _():
             for m in PIECES:
                 res = lone_row(m, (0, 1))
-                tr[0, pl.ds(m, CHUNK), :] = res[:, :LANES]
-                tr[1, pl.ds(m, CHUNK), :] = res[:, LANES:]
+                zo[0, pl.ds(OLAST * OROW + m, CHUNK), :] = res[:, :LANES]
+                zo[1, pl.ds(OLAST * OROW + m, CHUNK), :] = res[:, LANES:]
 
     mean2, inv2, fin2 = pair_layer(1, second_ahead, h2_near, h2_far, second_meanwhile)
     coef2 = save_coef(1, LANES, mean2, inv2, nav[1, 0:1], nav[1, 1:2])
@@ -406,8 +404,12 @@
                 work(m)
             lhs = join(lhs_of(m))
             res = mm(lhs, w_val)
-            dst[0, i, pl.ds(m, CHUNK), :] = res[:, :LANES]
-            dst[1, i, pl.ds(m, CHUNK), :] = res[:, LANES:]
+            for h in range(2):
+                part = res[:, LANES * h:LANES * h + LANES]
+                if dst is zo:
+                    zo[h, pl.ds(i * OROW + m, CHUNK), :] = part
+                else:
+                    dst[h, i, pl.ds(m, CHUNK), :] = part
             r3 = res.reshape(SUB, 8, WIDE)
             s1 = s1 + sublane_sum(r3)
             s2 = s2 + sublane_sum(r3 * r3)
@@ -453,7 +455,7 @@
             for m in PIECES:
                 res = lone_row(m, (2,))
                 for b, plane, off in ((0, 1, m), (1, 0, NIM + m)):
-                    z = tr[b, pl.ds(m, CHUNK), :] + res[:, LANES * b:LANES * b + LANES]
+                    z = zo[b, pl.ds(OLAST * OROW + m, CHUNK), :] + res[:, LANES * b:LANES * b + LANES]
                     yy[plane, FAR_SLOT, pl.ds(off, CHUNK), :] = normalise(z, *par)
 
 
@@ -472,7 +474,7 @@
         step = lax.rem(r - flip + OROWS, OROWS)
         for h in range(2):
             par = load_coef(coef3, LANES * h)
-            y3[r + 1, pl.ds(NIM + m, size), pl.ds(LANES * h, LANES)] = normalise(zo[h, step, pl.ds(m, size), :], *par)
+            y3[r + 1, pl.ds(NIM + m, size), pl.ds(LANES * h, LANES)] = normalise(zo[h, pl.ds(pl.multiple_of(step * OROW, NIM) + m, size), :], *par)
 
     def norm3(r):
         norm3_piece(r, 0, OROW)
@@ -609,10 +611,9 @@
             out_specs=(pl.BlockSpec(memory_space=pltpu.VMEM),) * 2,
             scratch_shapes=[
                 pltpu.VMEM((12, NIM, COLS, LANES), BF16),
-                pltpu.VMEM((NTR, NIM * COLS, LANES), F32),
                 pltpu.VMEM((2, ROWS + 2, YROW, LANES), BF16),
                 pltpu.VMEM((2, ROWS, MROW, LANES), F32),
-                pltpu.VMEM((2, OROWS, OROW, LANES), F32),
+                pltpu.VMEM((2, OROWS * OROW, LANES), F32),
                 pltpu.VMEM((OROWS + 2, O3ROW, WIDE), BF16),
                 pltpu.VMEM((2, YROW, LANES), BF16),
                 pltpu.VMEM((2, YROW, LANES), BF16),

time: 65.2 us -> 64.9 us (level)
  no operation moved by 1% of the time
where the time goes in v6:
time: 64.9 us
  Pallas kernels  64.7 us (100%)
    pallas_call x1, Pallas kernels, local_stack(): pl.pallas_call(kernel, out_shape=(pltpu.VMEM((2, OROWS, OROW, LANES), F32...  62.3 us
    pallas_call x1, Pallas kernels, local_stack(): pl.pallas_call(result_kernel, out_shape=jax.ShapeDtypeStruct((OROWS, OROW...  2.36 us

profile of v6, /device:TPU:0, one launch (start us, length us, event | category | flops | bytes accessed | tf_op | source)
XLA Modules:
  0.0 64.9 jit_solution(13986941999842642047)
XLA Ops:
  0.0 62.3 %shard_map.73 = (f32[2,6,1344,128]{3,2,1,0:T(8,128)S(1)}, f32[8,256]{1,0:T(8,128)S(1)}) custom-call(bf16[16,12,168,128]{3,2,1,0:T(8,128)(2,1)} %x_ref.1, bf16[2,3,384,128]{3,2,1,0:T(8,128)(2,1)} %bitcast.6, f32[2,2,128]{2,1,0:T(2,128)} %na_ref.1, bf16[3,3,128,256]{3,2,1,0:T(8,128)(2,1)} %wd_ref.1, f32[2,256]{1,0:T(2,128)} %nd_ref.1, ...), custom_call_target="tpu_custom_call" | custom-call | tf_op jit(solution)/shard_map/pallas_call | solution.py:607
  62.3 2.4 %shard_map.74 = bf16[6,1344,256]{2,1,0:T(8,128)(2,1)} custom-call(f32[2,6,1344,128]{3,2,1,0:T(8,128)S(1)} %get-tuple-element.7.z_ref, f32[8,256]{1,0:T(8,128)S(1)} %get-tuple-element.8.c_ref), custom_call_target="tpu_custom_call" | custom-call | tf_op jit(solution)/shard_map/pallas_call | solution.py:639
